TPU v7x, 32 devices: a whole 2x2x4 slice. The times are simulated.
32 devices in a mesh: af: 16 (over z, y, x), sa: 2 (over core).
Axes of the slice: x: 2, y: 2, z: 4, core: 2. Of those that a mesh axis runs over, the one named last changes fastest.
Arguments:
- series: float32 [8, 262144], P('sa', 'af'), parts along dimension 0, may hold values from -48 to 48
- tapers: float32 [10, 262144], P(None, 'af'), may hold values from -16 to 16
- concentration: float32 [10], replicated, may hold values from 0.2 to 0.95
- qi_weights: float32 [4, 10, 10], replicated, may hold values from -0.625 to 0.625
Outputs:
- spectrum: float32 [8, 16, 16384], P('sa', 'af'), parts along dimension 0
- qi_terms: float32 [8, 4, 16, 16384], P('sa', None, 'af'), parts along dimension 0
There are 2 independent parts, one for each index of `sa`. A program takes and returns all parts, laid end to end along the dimension named above; an argument that names none is the same for every part. Nothing has to cross between parts.
All inputs are finite; a program needn't handle non-finite values.
Results may differ from a plain program's by a relative error of at most 0.0001.
Values sent between devices are 32-bit elements; how exact they have to be, the bound alone decides.
A program may use at most 128 MiB of HBM per device.

v0:
```python
import functools
import math

import jax
import jax.numpy as jnp
import numpy as np
from jax import lax
from jax.experimental import pallas as pl
from jax.experimental.pallas import tpu as pltpu
from jax.sharding import PartitionSpec as P

ITERS = 3
LANES = 128
CHUNK = 16


def add(a, b):
    if a is None:
        return b
    return a if b is None else a + b


def sub(a, b):
    if b is None:
        return a
    return -b if a is None else a - b


def butterfly(values):
    n = len(values)
    if n == 1:
        return values
    even, odd = butterfly(values[0::2]), butterfly(values[1::2])
    low, high = [], []
    for k in range(n // 2):
        (er, ei), (tr, ti) = even[k], odd[k]
        if 4 * k == n:
            tr, ti = ti, (None if tr is None else -tr)
        elif k:
            c, s = math.cos(2 * math.pi * k / n), math.sin(2 * math.pi * k / n)
            if ti is None:
                tr, ti = tr * c, tr * (-s)
            else:
                tr, ti = tr * c + ti * s, ti * c - tr * s
        low.append((add(er, tr), add(ei, ti)))
        high.append((sub(er, tr), sub(ei, ti)))
    return low + high


def front_kernel(series_ref, tapers_ref, twist_ref, out_ref):
    shards, tapers = tapers_ref.shape[0], tapers_ref.shape[1]

    def body(k, carry):
        got = [(series_ref[p, 0] * tapers_ref[p, k], None) for p in range(shards)]
        for q, (re, im) in enumerate(butterfly(got)):
            c, s = twist_ref[0, q], twist_ref[1, q]
            if im is None:
                out_ref[q, 0, 0, k], out_ref[q, 1, 0, k] = re * c, re * (-s)
            else:
                out_ref[q, 0, 0, k] = re * c + im * s
                out_ref[q, 1, 0, k] = im * c - re * s
        return carry

    lax.fori_loop(0, tapers, body, 0)


def split(x):
    high = x.astype(jnp.bfloat16)
    return high, (x - high.astype(jnp.float32)).astype(jnp.bfloat16)


def dot3(a, b):
    dot = functools.partial(jnp.dot, preferred_element_type=jnp.float32)
    return dot(a[0], b[0]) + (dot(a[0], b[1]) + dot(a[1], b[0]))


def refine(estimate, powers, keep, variance):
    top = bottom = None
    for k, power in enumerate(powers):
        base = keep[k] * estimate + (1.0 - keep[k]) * variance
        weight = keep[k] / (base * base)
        top = add(top, weight * power)
        bottom = add(bottom, weight)
    return top / bottom


def back_kernel(keep_ref, pair_ref, var_ref, recv_ref, left_ref, right_ref, inner_ref,
                power_ref, est_ref, qi_ref, spec, qi):
    tapers = recv_ref.shape[3]
    rows = spec.shape[2]
    terms = qi.shape[0]
    left = (left_ref[0], left_ref[1])
    right = (right_ref[0], right_ref[1])

    def transform(k, carry):
        re = recv_ref[:, 0, 0, k].reshape(rows, LANES)
        im = recv_ref[:, 1, 0, k].reshape(rows, LANES)
        mid = dot3(left, split(jnp.concatenate([re, im], axis=0)))
        mr, mi = mid[:rows], mid[rows:]
        c, s = inner_ref[0], inner_ref[1]
        turned = jnp.concatenate([mr * c + mi * s, mi * c - mr * s], axis=1)
        done = dot3(split(turned), right)
        spec[0, k] = done[:, :LANES]
        spec[1, k] = done[:, LANES:]
        return carry

    lax.fori_loop(0, tapers, transform, 0)
    variance = var_ref[pl.program_id(0)]
    keep = [keep_ref[k] for k in range(tapers)]

    def combine(i, carry):
        at = pl.ds(pl.multiple_of(i * CHUNK, CHUNK), CHUNK)
        re = [spec[0, k, at] for k in range(tapers)]
        im = [spec[1, k, at] for k in range(tapers)]
        sums = [None] * terms
        powers = []
        pair = 0
        for j in range(tapers):
            for k in range(j, tapers):
                both = re[j] * re[k] + im[j] * im[k]
                if j == k:
                    powers.append(both)
                    power_ref[0, j, at] = both
                for t in range(terms):
                    sums[t] = add(sums[t], pair_ref[t, pair] * both)
                pair += 1
        for t in range(terms):
            qi[t, at] = sums[t]
        est_ref[0, at] = refine(0.5 * (powers[0] + powers[1]), powers, keep, variance)
        return carry

    lax.fori_loop(0, rows // CHUNK, combine, 0)
    for t in range(terms):
        qi_ref[0, t] = qi[t].T


def sweep_kernel(last, keep_ref, var_ref, power_ref, est_ref, out_ref, hold):
    tapers, rows = power_ref.shape[1], power_ref.shape[2]
    variance = var_ref[pl.program_id(0)]
    keep = [keep_ref[k] for k in range(tapers)]

    def body(i, carry):
        at = pl.ds(pl.multiple_of(i * CHUNK, CHUNK), CHUNK)
        powers = [power_ref[0, k, at] for k in range(tapers)]
        hold[at] = refine(est_ref[0, at], powers, keep, variance)
        return carry

    lax.fori_loop(0, rows // CHUNK, body, 0)
    out_ref[0] = hold[...].T if last else hold[...]


def total_kernel(part_ref, out_ref, slots, send_sem, recv_sem):
    shards = slots.shape[0]
    me = lax.axis_index("af")
    barrier = pltpu.get_barrier_semaphore()
    peers = [lax.rem(me + d, shards) for d in range(shards)]
    for peer in peers[1:]:
        pl.semaphore_signal(
            barrier, inc=1, device_id={"af": peer}, device_id_type=pl.DeviceIdType.MESH
        )
    pl.semaphore_wait(barrier, shards - 1)
    copies = []
    for d in range(1, shards):
        copy = pltpu.make_async_remote_copy(
            src_ref=part_ref,
            dst_ref=slots.at[d],
            send_sem=send_sem.at[d],
            recv_sem=recv_sem.at[d],
            device_id={"af": peers[d]},
            device_id_type=pl.DeviceIdType.MESH,
        )
        copy.start()
        copies.append(copy)
    total = part_ref[...]
    for d, copy in enumerate(copies, 1):
        copy.wait()
        total += slots[d]
    out_ref[...] = total


def total_over_devices(part, shards, ident):
    vmem = pl.BlockSpec(memory_space=pltpu.VMEM)
    return pl.pallas_call(
        total_kernel,
        out_shape=jax.ShapeDtypeStruct(part.shape, part.dtype),
        in_specs=[vmem],
        out_specs=vmem,
        scratch_shapes=[
            pltpu.VMEM((shards,) + part.shape, part.dtype),
            pltpu.SemaphoreType.DMA((shards,)),
            pltpu.SemaphoreType.DMA((shards,)),
        ],
        compiler_params=pltpu.CompilerParams(collective_id=ident, has_side_effects=True),
    )(part)


def whole(shape):
    return pl.BlockSpec(shape, lambda i: (0,) * len(shape))


def each(shape, axis):
    return pl.BlockSpec(shape, lambda i: tuple(i if d == axis else 0 for d in range(len(shape))))


def smem():
    return pl.BlockSpec(memory_space=pltpu.SMEM)


def complex_table(n, left):
    angle = 2 * np.pi * (np.outer(np.arange(n), np.arange(n)) % n) / n
    c, s = np.cos(angle), np.sin(angle)
    full = np.block([[c, s], [-s, c]])
    full = jnp.asarray((full if left else full.T).astype(np.float32))
    return jnp.stack(split(full))


def phase(a, b, modulus):
    angles = (a * b % modulus).astype(jnp.float32) * (2.0 * math.pi / modulus)
    return jnp.stack([jnp.cos(angles), jnp.sin(angles)])


def local(series, tapers, concentration, qi_weights):
    shards = lax.axis_size("af")
    rank = lax.axis_index("af")
    count, local_len = series.shape
    taper_count = tapers.shape[0]
    terms = qi_weights.shape[0]
    block_len = local_len // shards
    sub_rows = block_len // LANES
    rows = local_len // LANES
    length_all = local_len * shards
    f32 = jnp.float32

    scaled = series * (1.0 / math.sqrt(length_all))
    energy = 0.5 * jnp.sum((scaled * tapers[:1]) ** 2 + (scaled * tapers[1:2]) ** 2, axis=1)
    energy_row = jnp.tile(jnp.pad(energy, (0, LANES - count)), rows)[None]
    both = jnp.concatenate([scaled, tapers, energy_row], axis=0)
    both = both.reshape(count + taper_count + 1, shards, sub_rows, LANES).transpose(1, 0, 2, 3)
    got = lax.all_to_all(both, "af", split_axis=0, concat_axis=0, tiled=True)
    got_series, got_tapers = got[:, :count], got[:, count:-1]
    variance = jnp.sum(got[:, -1, 0, :count], axis=0)

    pos = rank * block_len + jnp.arange(block_len, dtype=jnp.int32)
    twist = phase(jnp.arange(shards, dtype=jnp.int32)[:, None], pos[None, :], length_all)
    twist = twist.reshape(2, shards, sub_rows, LANES)
    turned = pl.pallas_call(
        front_kernel,
        grid=(count,),
        out_shape=jax.ShapeDtypeStruct((shards, 2, count, taper_count, sub_rows, LANES), f32),
        in_specs=[
            each((shards, 1, sub_rows, LANES), 1),
            whole((shards, taper_count, sub_rows, LANES)),
            whole((2, shards, sub_rows, LANES)),
        ],
        out_specs=each((shards, 2, 1, taper_count, sub_rows, LANES), 2),
    )(got_series, got_tapers, twist)
    recv = lax.all_to_all(turned, "af", split_axis=0, concat_axis=0, tiled=True)

    inner = phase(
        jnp.arange(rows, dtype=jnp.int32)[:, None],
        jnp.arange(LANES, dtype=jnp.int32)[None, :],
        local_len,
    )
    symmetric = qi_weights + qi_weights.transpose(0, 2, 1)
    pairs = jnp.stack(
        [
            qi_weights[:, j, j] if j == k else symmetric[:, j, k]
            for j in range(taper_count)
            for k in range(j, taper_count)
        ],
        axis=1,
    )
    plane = (1, rows, LANES)
    flat = (1, LANES, rows)
    powers, estimate, qi_terms = pl.pallas_call(
        back_kernel,
        grid=(count,),
        out_shape=(
            jax.ShapeDtypeStruct((count, taper_count, rows, LANES), f32),
            jax.ShapeDtypeStruct((count, rows, LANES), f32),
            jax.ShapeDtypeStruct((count, terms, LANES, rows), f32),
        ),
        in_specs=[
            smem(),
            smem(),
            smem(),
            each((shards, 2, 1, taper_count, sub_rows, LANES), 2),
            whole((2, 2 * rows, 2 * rows)),
            whole((2, 2 * LANES, 2 * LANES)),
            whole((2, rows, LANES)),
        ],
        out_specs=(
            each((1, taper_count, rows, LANES), 0),
            each(plane, 0),
            each((1, terms, LANES, rows), 0),
        ),
        scratch_shapes=[
            pltpu.VMEM((2, taper_count, rows, LANES), f32),
            pltpu.VMEM((terms, rows, LANES), f32),
        ],
    )(
        concentration, pairs, variance, recv, complex_table(rows, True), complex_table(LANES, False), inner
    )
    for sweep in range(1, ITERS):
        sums = total_over_devices(jnp.sum(estimate, axis=1), shards, sweep)
        variance = jnp.sum(sums, axis=1) / length_all
        last = sweep == ITERS - 1
        shape = flat if last else plane
        estimate = pl.pallas_call(
            functools.partial(sweep_kernel, last),
            grid=(count,),
            out_shape=jax.ShapeDtypeStruct((count,) + shape[1:], f32),
            in_specs=[smem(), smem(), each((1, taper_count, rows, LANES), 0), each(plane, 0)],
            out_specs=each(shape, 0),
            scratch_shapes=[pltpu.VMEM((rows, LANES), f32)],
        )(concentration, variance, powers, estimate)
    return (
        estimate.reshape(count, 1, local_len),
        qi_terms.reshape(count, terms, 1, local_len),
    )


def solution(mesh):
    placed = (P("sa", "af"), P(None, "af"), P(), P())
    return jax.shard_map(
        local,
        mesh=mesh,
        in_specs=placed,
        out_specs=(P("sa", "af", None), P("sa", None, "af", None)),
        check_vma=False,
    )
```

profile of v0, /device:TPU:0, one launch (start us, length us, event | category | flops | bytes accessed | tf_op | source)
XLA Modules:
  0.0 227.7 jit_solution(2784604995735585082)
XLA Ops:
  0.6 1.3 slice_multiply_fusion.1
  1.9 1.2 multiply_bitcast_fusion
  3.2 1.4 copy.127
  4.7 1.0 maximum_bitcast_fusion
  5.7 8.3 %all-to-all-start = ((f32[16,15,8,128]{3,2,1,0:T(8,128)}), f32[16,15,8,128]{3,2,1,0:T(8,128)S(1)}, u32[]{:S(2)}, u32[]{:S(2)}) async-start(f32[16,15,8,128]{3,2,1,0:T(8,128)} %maximum_bitcast_fusion), calls=%async_computation | async-start | bytes 1966080 | tf_op jit(solution)/shard_map/all_to_all | solution.py:239
  14.0 0.3 fusion.15
  14.3 0.6 pad_maximum_fusion.twist_ref
  15.0 22.2 %all-to-all-done = f32[16,15,8,128]{3,2,1,0:T(8,128)S(1)} async-done(((f32[16,15,8,128]{3,2,1,0:T(8,128)}), f32[16,15,8,128]{3,2,1,0:T(8,128)S(1)}, u32[]{:S(2)}, u32[]{:S(2)}) %all-to-all-start) | async-done | bytes 983072 | tf_op jit(solution)/shard_map/all_to_all | solution.py:239
  37.1 0.7 slice.286.series_ref
  37.9 0.9 slice.287.tapers_ref
  38.8 5.0 %shard_map.77 = f32[16,2,4,10,8,128]{5,4,3,2,1,0:T(8,128)} custom-call(f32[16,4,8,128]{3,2,1,0:T(8,128)} %slice.286.series_ref, f32[16,10,8,128]{3,2,1,0:T(8,128)} %slice.287.tapers_ref, f32[2,16,8,128]{3,2,1,0:T(8,128)} %pad_maximum_fusion.twist_ref), custom_call_target="tpu_custom_call" | custom-call | tf_op jit(solution)/shard_map/pallas_call | solution.py:246
  43.8 0.0 copy-start
  43.8 5.9 %all-to-all-start.1 = ((f32[16,2,4,10,8,128]{5,4,3,2,1,0:T(8,128)}), f32[16,2,4,10,8,128]{5,4,3,2,1,0:T(8,128)}, u32[]{:S(2)}, u32[]{:S(2)}) async-start(f32[16,2,4,10,8,128]{5,4,3,2,1,0:T(8,128)} %shard_map.77), calls=%async_computation.1 | async-start | bytes 10485760 | tf_op jit(solution)/shard_map/all_to_all | solution.py:257
  49.7 0.0 copy-done
  49.7 0.1 copy.66
  49.8 0.1 slice_bitcast_fusion.39
  49.9 0.1 slice_bitcast_fusion.20
  50.0 0.1 slice_bitcast_fusion.1
  50.1 0.8 stack.31.pair_ref
  50.9 0.3 fusion.12
  51.1 0.7 pad_maximum_fusion.1.inner_ref
  51.8 0.6 slice_reduce_fusion.var_ref
  52.3 93.5 %all-to-all-done.1.recv_ref = f32[16,2,4,10,8,128]{5,4,3,2,1,0:T(8,128)} async-done(((f32[16,2,4,10,8,128]{5,4,3,2,1,0:T(8,128)}), f32[16,2,4,10,8,128]{5,4,3,2,1,0:T(8,128)}, u32[]{:S(2)}, u32[]{:S(2)}) %all-to-all-start.1) | async-done | bytes 5242912 | tf_op jit(solution)/shard_map/all_to_all | solution.py:257
  145.8 30.9 %shard_map.78 = (f32[4,10,128,128]{3,2,1,0:T(8,128)}, f32[4,128,128]{2,1,0:T(8,128)}, f32[4,4,128,128]{3,2,1,0:T(8,128)}) custom-call(f32[10]{0:T(128)} %keep_ref.5, f32[4,55]{1,0:T(4,128)} %stack.31.pair_ref, f32[4]{0:T(128)} %slice_reduce_fusion.var_ref, f32[16,2,4,10,8,128]{5,4,3,2,1,0:T(8,128)} %all-to-all-done.1.recv_ref, ...), custom_call_target="tpu_custom_call" | custom-call | tf_op jit(solution)/shard_map/pallas_call | solution.py:275
  176.8 1.6 reduce_sum.56.part_ref
  178.3 27.9 %shard_map.79 = f32[4,128]{1,0:T(4,128)} custom-call(f32[4,128]{1,0:T(4,128)} %reduce_sum.56.part_ref), custom_call_target="tpu_custom_call" | custom-call | tf_op jit(solution)/shard_map/pallas_call | solution.py:183
  206.2 0.8 reduce_sum.57
  207.0 0.6 broadcast_multiply_fusion.1.var_ref
  207.6 4.1 %shard_map.80.est_ref = f32[4,128,128]{2,1,0:T(8,128)} custom-call(f32[10]{0:T(128)} %keep_ref.5, f32[4]{0:T(128)} %broadcast_multiply_fusion.1.var_ref, f32[4,10,128,128]{3,2,1,0:T(8,128)} %get-tuple-element.6.power_ref, f32[4,128,128]{2,1,0:T(8,128)} %get-tuple-element.5.est_ref), custom_call_target="tpu_custom_call" | custom-call | tf_op jit(solution)/shard_map/pallas_call | solution.py:309
  211.6 1.6 reduce_sum.58.part_ref
  213.2 8.8 %shard_map.81 = f32[4,128]{1,0:T(4,128)} custom-call(f32[4,128]{1,0:T(4,128)} %reduce_sum.58.part_ref), custom_call_target="tpu_custom_call" | custom-call | tf_op jit(solution)/shard_map/pallas_call | solution.py:183
  222.0 0.8 reduce_sum.59
  222.8 0.6 broadcast_multiply_fusion.var_ref
  223.4 4.3 %shard_map.82 = f32[4,128,128]{2,1,0:T(8,128)} custom-call(f32[10]{0:T(128)} %keep_ref.5, f32[4]{0:T(128)} %broadcast_multiply_fusion.var_ref, f32[4,10,128,128]{3,2,1,0:T(8,128)} %get-tuple-element.6.power_ref, f32[4,128,128]{2,1,0:T(8,128)} %shard_map.80.est_ref), custom_call_target="tpu_custom_call" | custom-call | tf_op jit(solution)/shard_map/pallas_call | solution.py:309
  (6 shorter events, 0.1 us)
Async XLA Ops:
  5.7 31.5 %all-to-all-start = ((f32[16,15,8,128]{3,2,1,0:T(8,128)}), f32[16,15,8,128]{3,2,1,0:T(8,128)S(1)}, u32[]{:S(2)}, u32[]{:S(2)}) async-start(f32[16,15,8,128]{3,2,1,0:T(8,128)} %maximum_bitcast_fusion), calls=%async_computation | async-start | bytes 1966080 | tf_op jit(solution)/shard_map/all_to_all | solution.py:239
  43.8 5.9 %copy-start = (f32[4,10,10]{2,0,1:T(4,128)S(1)}, f32[4,10,10]{2,0,1:T(4,128)}, u32[]{:S(2)}) copy-start(f32[4,10,10]{2,0,1:T(4,128)} %param.9) | copy-start | bytes 4804
  43.8 102.0 %all-to-all-start.1 = ((f32[16,2,4,10,8,128]{5,4,3,2,1,0:T(8,128)}), f32[16,2,4,10,8,128]{5,4,3,2,1,0:T(8,128)}, u32[]{:S(2)}, u32[]{:S(2)}) async-start(f32[16,2,4,10,8,128]{5,4,3,2,1,0:T(8,128)} %shard_map.77), calls=%async_computation.1 | async-start | bytes 10485760 | tf_op jit(solution)/shard_map/all_to_all | solution.py:257
where the time goes:
time: 228 us
  waiting for transfers between devices  116 us (51%)
  Pallas kernels  81 us (36%)
  starting transfers between devices  14.3 us (6%)
  other arithmetic  11.8 us (5%)
  local copies, waits for them, and re-layouts  4.21 us (2%)
    all_to_all x1, waiting for transfers between devices, local(): recv = lax.all_to_all(turned, 'af', split_axis=0, concat_axis=0, tiled=True)  93.5 us
    pallas_call x2, Pallas kernels, total_over_devices(): pl.pallas_call(total_kernel, out_shape=jax.ShapeDtypeStruct(part.shape, p...  36.7 us
    pallas_call x1, Pallas kernels, local(): pl.pallas_call(back_kernel, grid=(count,), out_shape=(jax.ShapeDtypeStruc...  30.9 us
    all_to_all x1, waiting for transfers between devices, local(): got = lax.all_to_all(both, 'af', split_axis=0, concat_axis=0, tiled=True)  22.2 us
    pallas_call x2, Pallas kernels, local(): pl.pallas_call(functools.partial(sweep_kernel, last), grid=(count,), out_...  8.37 us
    all_to_all x1, starting transfers between devices, local(): got = lax.all_to_all(both, 'af', split_axis=0, concat_axis=0, tiled=True)  8.34 us
    all_to_all x1, starting transfers between devices, local(): recv = lax.all_to_all(turned, 'af', split_axis=0, concat_axis=0, tiled=True)  5.92 us
    pallas_call x1, Pallas kernels, local(): pl.pallas_call(front_kernel, grid=(count,), out_shape=jax.ShapeDtypeStruc...  5.02 us
  transfers between devices with their start and end apart: 2, of which 2 were waited for; matrix products, arithmetic and copies ran while one was open for 2% of the time, Pallas kernels for 0%

commit v1 on v0

v1 whole, which is shorter than its diff:
```python
import functools
import math

import jax
import jax.numpy as jnp
import numpy as np
from jax import lax
from jax.experimental import pallas as pl
from jax.experimental.pallas import tpu as pltpu
from jax.sharding import PartitionSpec as P

ITERS = 3
LANES = 128
CHUNK = 16
MESH = pl.DeviceIdType.MESH


def add(a, b):
    if a is None:
        return b
    return a if b is None else a + b


def sub(a, b):
    if b is None:
        return a
    return -b if a is None else a - b


def butterfly(values):
    n = len(values)
    if n == 1:
        return values
    even, odd = butterfly(values[0::2]), butterfly(values[1::2])
    low, high = [], []
    for k in range(n // 2):
        (er, ei), (tr, ti) = even[k], odd[k]
        if 4 * k == n:
            tr, ti = ti, (None if tr is None else -tr)
        elif k:
            c, s = math.cos(2 * math.pi * k / n), math.sin(2 * math.pi * k / n)
            if ti is None:
                tr, ti = tr * c, tr * (-s)
            else:
                tr, ti = tr * c + ti * s, ti * c - tr * s
        low.append((add(er, tr), add(ei, ti)))
        high.append((sub(er, tr), sub(ei, ti)))
    return low + high


def split(x):
    high = x.astype(jnp.bfloat16)
    return high, (x - high.astype(jnp.float32)).astype(jnp.bfloat16)


def dot3(a, b):
    dot = functools.partial(jnp.dot, preferred_element_type=jnp.float32)
    return dot(a[0], b[0]) + (dot(a[0], b[1]) + dot(a[1], b[0]))


def refine(estimate, powers, keep, variance):
    top = bottom = None
    for k, power in enumerate(powers):
        base = keep[k] * estimate + (1.0 - keep[k]) * variance
        weight = keep[k] / (base * base)
        top = add(top, weight * power)
        bottom = add(bottom, weight)
    return top / bottom


def turn(index, period):
    if period & (period - 1):
        index = lax.rem(index, jnp.full_like(index, period))
    else:
        index = index & (period - 1)
    angle = index.astype(jnp.float32) * (2.0 * math.pi / period)
    return jnp.cos(angle), jnp.sin(angle)


def flip(x):
    rows, lanes = x.shape
    lane = lanes - 1 - lax.broadcasted_iota(jnp.int32, (8, lanes), 1)
    line = 7 - lax.broadcasted_iota(jnp.int32, (8, lanes), 0)
    parts = []
    for i in reversed(range(rows // 8)):
        part = jnp.take_along_axis(x[8 * i : 8 * i + 8], lane, axis=1)
        parts.append(jnp.take_along_axis(part, line, axis=0))
    return jnp.concatenate(parts, axis=0)


def remote(src, dst, send, recv, where):
    return pltpu.make_async_remote_copy(
        src_ref=src, dst_ref=dst, send_sem=send, recv_sem=recv, device_id=where, device_id_type=MESH
    )


def fused_kernel(
    n, cores, series_ref, tapers_ref, keep_ref, mix_ref, spec_ref, qi_ref,
    ser, tap, zbuf, recv, en_out, en_in, sum_out, sum_in, left, right, inner, weigh,
    spec, power, est, qi, spec_out, qi_out, pairs, folded,
    ser_ss, ser_rs, tap_ss, tap_rs, core_ss, core_rs, en_ss, en_rs, z_ss, z_rs,
    sum_ss, sum_rs, qo_ss, qo_rs, so_ss, so_rs,
):
    half = n // 2
    count, sub_rows = series_ref.shape[0], series_ref.shape[2]
    mine = count // 2
    tapers, terms = tap.shape[1], mix_ref.shape[0]
    group = tapers // cores
    rows = half * sub_rows
    tall = spec.shape[2]
    extra = tall - rows
    local_len = rows * LANES
    length_all = local_len * n
    f32 = jnp.float32
    me, core = lax.axis_index("af"), lax.axis_index("sa")
    g, h = me // half, lax.rem(me, half)
    peers = [(dg, dh) for dg in (1, 0) for dh in range(half) if dg or dh]
    single = h == 0

    def ahead(dg, dh):
        return lax.rem(g + dg, 2), lax.rem(h + dh, half)

    def behind(dg, dh):
        return lax.rem(g + dg, 2), lax.rem(h + half - dh, half)

    def flat(at):
        return at[0] * half + at[1]

    def friend(dh):
        return {"af": g * half + lax.rem(h + dh, half)}

    partner = {"af": (1 - g) * half + lax.rem(half - h, half)}
    other_core = lax.rem(core + 1, cores)

    barrier = pltpu.get_barrier_semaphore()
    for dg, dh in peers:
        pl.semaphore_signal(barrier, inc=1, device_id={"af": flat(ahead(dg, dh))}, device_id_type=MESH)
    pl.semaphore_signal(barrier, inc=1, device_id={"sa": other_core}, device_id_type=MESH)
    pl.semaphore_wait(barrier, n)

    def ser_copy(dg, dh):
        to = ahead(dg, dh)
        return remote(
            series_ref.at[pl.ds(to[0] * mine, mine), to[1]], ser.at[me],
            ser_ss.at[dg, dh], ser_rs.at[dg, dh], {"af": flat(to)},
        )

    def tap_copy(dg, dh):
        to = ahead(dg, dh)
        own = pl.ds(core * group, group)
        return remote(
            tapers_ref.at[own, to[1]], tap.at[me, own],
            tap_ss.at[dg, dh], tap_rs.at[dg, dh], {"af": flat(to)},
        )

    def core_copy(dg, dh):
        at = tap.at[flat(behind(dg, dh)), pl.ds(core * group, group)]
        return remote(at, at, core_ss.at[dg, dh], core_rs.at[dg, dh], {"sa": other_core})

    for dg, dh in peers:
        tap_copy(dg, dh).start()
        ser_copy(dg, dh).start()

    for s in range(mine):
        ser[me, s] = series_ref[g * mine + s, h]
    for k in range(tapers):
        tap[me, k] = tapers_ref[k, h]
    for t in range(terms):
        p = 0
        for j in range(tapers):
            for k in range(j, tapers):
                value = mix_ref[t, j, k]
                pairs[t, p] = value if j == k else value + mix_ref[t, k, j]
                p += 1

    def frequency(shape):
        at = lax.broadcasted_iota(jnp.int32, shape, 0)
        upper = (at >= rows // 2) & (at < rows)
        class_of = jnp.where(single, jnp.where(upper, half, 0), me)
        line = jnp.where(at < rows, at, rows // 2)
        class_of = jnp.where(at < rows, class_of, 0)
        return n * line + class_of, at, upper

    freq, at, upper = frequency((tall, rows))
    c, s = turn(lax.broadcasted_iota(jnp.int32, (tall, rows), 1) * freq, rows * n)
    first = jnp.where(upper, 1, 0) == g
    inside = at < rows
    once = at == rows
    zero = jnp.zeros_like(c)
    take0 = jnp.where(single, jnp.where(inside | once, jnp.where(first, 1.0, 0.0), 0.0), jnp.where(inside, 1.0, 0.0))
    take1 = jnp.where(single, jnp.where(inside | once, jnp.where(first, 0.0, 1.0), 0.0), 0.0)
    plain = jnp.where(single, 0.0, jnp.where(inside, 1.0, 0.0))
    real0, real1 = c * take0, c * take1 + s * plain
    imag0, imag1 = -(s * take0), c * plain - s * take1
    full = jnp.concatenate(
        [
            jnp.concatenate([real0[:rows], real1[:rows]], axis=1),
            jnp.concatenate([imag0[:rows], imag1[:rows]], axis=1),
            jnp.concatenate([real0[rows:], real1[rows:]], axis=1),
        ],
        axis=0,
    )
    left[0], left[1] = split(full)

    freq, at, upper = frequency((tall, LANES))
    c, s = turn(lax.broadcasted_iota(jnp.int32, (tall, LANES), 1) * freq, length_all)
    scale = 1.0 / math.sqrt(length_all)
    inner[0], inner[1] = c * scale, s * scale
    weigh[...] = jnp.where(
        single,
        jnp.where(at < rows, jnp.where(at == 0, 1.0, 2.0), jnp.where(at == rows, 1.0, 0.0)),
        jnp.where(at < rows, 2.0, 0.0),
    )
    grid = (LANES, LANES)
    c, s = turn(lax.broadcasted_iota(jnp.int32, grid, 0) * lax.broadcasted_iota(jnp.int32, grid, 1), LANES)
    right[0], right[1] = split(
        jnp.concatenate([jnp.concatenate([c, -s], axis=1), jnp.concatenate([s, c], axis=1)], axis=0)
    )
    en_out[...] = jnp.zeros_like(en_out)
    sum_out[...] = jnp.zeros_like(sum_out)

    for dg, dh in peers:
        tap_copy(dg, dh).wait_recv()
        core_copy(dg, dh).start()
    for dg, dh in peers:
        ser_copy(dg, dh).wait_recv()
    for dg, dh in peers:
        core_copy(dg, dh).wait_recv()

    def energy(p, total):
        one, two = tap[p, 0], tap[p, 1]
        new = []
        for s in range(mine):
            a, b = ser[p, s] * one, ser[p, s] * two
            new.append(total[s] + (a * a + b * b))
        return tuple(new)

    total = lax.fori_loop(0, n, energy, tuple(jnp.zeros((sub_rows, LANES), f32) for _ in range(mine)))
    for s in range(mine):
        en_out[s : s + 1] = jnp.sum(total[s], axis=0, keepdims=True)

    def en_copy(dh):
        return remote(en_out, en_in.at[dh], en_ss.at[dh], en_rs.at[dh], friend(dh))

    for dh in range(1, half):
        en_copy(dh).start()

    def z_copy(s, dh):
        to = lax.rem(h + dh, half)
        return remote(
            zbuf.at[to, s], recv.at[s, :, :, h], z_ss.at[s, dh], z_rs.at[s, dh], friend(dh)
        )

    sign = (1 - 2 * g).astype(f32)
    tile = min(8, sub_rows)
    for s in range(mine):
        for i in range(sub_rows // tile):
            part = pl.ds(i * tile, tile)

            def front(k, carry, s=s, part=part):
                got = []
                for p in range(n):
                    value = ser[p, s, part] * tap[p, k, part]
                    got.append((value * sign if p % 2 else value, None))
                out = butterfly(got)
                for u in range(half):
                    re, im = out[u]
                    zbuf[u, s, k, 0, part] = re
                    zbuf[u, s, k, 1, part] = out[half][0] if u == 0 else im
                return carry

            lax.fori_loop(0, tapers, front, 0)
        for dh in range(1, half):
            z_copy(s, dh).start()
        for k in range(tapers):
            for part in range(2):
                recv[s, k, part, h] = zbuf[h, s, k, part]

    for dh in range(1, half):
        en_copy(dh).wait_recv()
    total = en_out[...]
    for dh in range(1, half):
        total += en_in[dh]
    variance0 = [jnp.sum(total[s : s + 1]) * (0.5 / length_all) for s in range(mine)]
    keep = [keep_ref[k] for k in range(tapers)]

    def sum_copy(s, it, dh):
        return remote(
            sum_out.at[s, it], sum_in.at[s, it, dh], sum_ss.at[s, it, dh], sum_rs.at[s, it, dh], friend(dh)
        )

    def share(s, it, total):
        sum_out[s, it, 0:1] = jnp.sum(total, axis=0, keepdims=True)
        for dh in range(1, half):
            sum_copy(s, it, dh).start()

    def collect(s, it):
        total = sum_out[s, it]
        for dh in range(1, half):
            sum_copy(s, it, dh).wait_recv()
            total += sum_in[s, it, dh]
        return jnp.sum(total) / length_all

    def transform(s):
        def body(kk, carry):
            k = 2 * kk
            x = jnp.concatenate(
                [recv[s, k].reshape(2 * rows, LANES), recv[s, k + 1].reshape(2 * rows, LANES)], axis=1
            )
            mid = dot3((left[0], left[1]), split(x))
            c, d = inner[0], inner[1]
            turned = []
            for i in range(2):
                lanes = slice(i * LANES, (i + 1) * LANES)
                mr = jnp.concatenate([mid[:rows, lanes], mid[2 * rows :, lanes]], axis=0)
                mi = jnp.concatenate([mid[rows : 2 * rows, lanes], jnp.zeros((extra, LANES), f32)], axis=0)
                turned.append(jnp.concatenate([mr * c + mi * d, mi * c - mr * d], axis=1))
            done = dot3(split(jnp.concatenate(turned, axis=0)), (right[0], right[1]))
            for i in range(2):
                block = done[i * tall : (i + 1) * tall]
                spec[0, k + i] = block[:, :LANES]
                spec[1, k + i] = block[:, LANES:]
            return carry

        lax.fori_loop(0, tapers // 2, body, 0)

    def combine(s, variance):
        def body(i, total):
            at = pl.ds(pl.multiple_of(i * CHUNK, CHUNK), CHUNK)
            re = [spec[0, k, at] for k in range(tapers)]
            im = [spec[1, k, at] for k in range(tapers)]
            sums = [None] * terms
            powers = []
            pair = 0
            for j in range(tapers):
                for k in range(j, tapers):
                    both = re[j] * re[k] + im[j] * im[k]
                    if j == k:
                        powers.append(both)
                        power[s, k, at] = both
                    for t in range(terms):
                        sums[t] = add(sums[t], pairs[t, pair] * both)
                    pair += 1
            for t in range(terms):
                qi[s, t, at] = sums[t]
            new = refine(0.5 * (powers[0] + powers[1]), powers, keep, variance)
            est[s, at] = new
            return total + new * weigh[at]

        return lax.fori_loop(0, tall // CHUNK, body, jnp.zeros((CHUNK, LANES), f32))

    def sweep(s, variance):
        def body(i, total):
            at = pl.ds(pl.multiple_of(i * CHUNK, CHUNK), CHUNK)
            new = refine(est[s, at], [power[s, k, at] for k in range(tapers)], keep, variance)
            est[s, at] = new
            return total + new * weigh[at]

        return lax.fori_loop(0, tall // CHUNK, body, jnp.zeros((CHUNK, LANES), f32))

    def assemble(src):
        mirrored = flip(src[0:rows])

        @pl.when(jnp.logical_not(single))
        def _():
            folded[0] = src[0:rows]
            folded[1] = mirrored

        @pl.when(single)
        def _():
            folded[g, 0 : rows // 2] = src[0 : rows // 2]
            folded[g, rows // 2 : rows // 2 + 1] = src[rows : rows + 1]
            folded[g, rows // 2 + 1 : rows] = mirrored[rows // 2 : rows - 1]
            folded[1 - g, 0 : rows // 2] = mirrored[: rows // 2]
            folded[1 - g, rows // 2 : rows] = src[rows // 2 : rows]

        return folded[0].T, folded[1].T

    def qi_copy(s):
        return remote(qi_out.at[s], qi_ref.at[g * mine + s], qo_ss.at[s], qo_rs.at[s], partner)

    def spec_copy(s):
        return remote(spec_out.at[s], spec_ref.at[g * mine + s], so_ss.at[s], so_rs.at[s], partner)

    def outputs_qi(s):
        for t in range(terms):
            own, sent = assemble(qi.at[s, t])
            qi_ref[g * mine + s, t] = own
            qi_out[s, t] = sent
        qi_copy(s).start()

    def outputs_spec(s):
        own, sent = assemble(est.at[s])
        spec_ref[g * mine + s] = own
        spec_out[s] = sent
        spec_copy(s).start()

    for s in range(mine):
        for dh in range(1, half):
            z_copy(s, dh).wait_recv()
        transform(s)
        share(s, 0, combine(s, variance0[s]))
        outputs_qi(s)
        for it in range(1, ITERS):
            total = sweep(s, collect(s, it - 1))
            if it < ITERS - 1:
                share(s, it, total)
        outputs_spec(s)

    for s in range(mine):
        qi_copy(s).wait_recv()
        spec_copy(s).wait_recv()
        qi_copy(s).wait_send()
        spec_copy(s).wait_send()
        for dh in range(1, half):
            z_copy(s, dh).wait_send()
            for it in range(ITERS - 1):
                sum_copy(s, it, dh).wait_send()
    for dh in range(1, half):
        en_copy(dh).wait_send()
    for dg, dh in peers:
        tap_copy(dg, dh).wait_send()
        ser_copy(dg, dh).wait_send()
        core_copy(dg, dh).wait_send()


def local(cores, series, tapers, concentration, qi_weights):
    n = lax.axis_size("af")
    count, local_len = series.shape
    taper_count = tapers.shape[0]
    terms = qi_weights.shape[0]
    half, mine = n // 2, count // 2
    sub_rows = local_len // (half * LANES)
    rows = local_len // LANES
    tall = rows + CHUNK
    f32 = jnp.float32
    bf16 = jnp.bfloat16
    vmem = pl.BlockSpec(memory_space=pltpu.VMEM)
    smem = pl.BlockSpec(memory_space=pltpu.SMEM)
    dma = pltpu.SemaphoreType.DMA
    spectrum, qi_terms = pl.pallas_call(
        functools.partial(fused_kernel, n, cores),
        out_shape=(
            jax.ShapeDtypeStruct((count, LANES, rows), f32),
            jax.ShapeDtypeStruct((count, terms, LANES, rows), f32),
        ),
        in_specs=[vmem, vmem, smem, smem],
        out_specs=(vmem, vmem),
        scratch_shapes=[
            pltpu.VMEM((n, mine, sub_rows, LANES), f32),
            pltpu.VMEM((n, taper_count, sub_rows, LANES), f32),
            pltpu.VMEM((half, mine, taper_count, 2, sub_rows, LANES), f32),
            pltpu.VMEM((mine, taper_count, 2, half, sub_rows, LANES), f32),
            pltpu.VMEM((8, LANES), f32),
            pltpu.VMEM((half, 8, LANES), f32),
            pltpu.VMEM((mine, ITERS - 1, 8, LANES), f32),
            pltpu.VMEM((mine, ITERS - 1, half, 8, LANES), f32),
            pltpu.VMEM((2, rows + tall, 2 * rows), bf16),
            pltpu.VMEM((2, 2 * LANES, 2 * LANES), bf16),
            pltpu.VMEM((2, tall, LANES), f32),
            pltpu.VMEM((tall, LANES), f32),
            pltpu.VMEM((2, taper_count, tall, LANES), f32),
            pltpu.VMEM((mine, taper_count, tall, LANES), f32),
            pltpu.VMEM((mine, tall, LANES), f32),
            pltpu.VMEM((mine, terms, tall, LANES), f32),
            pltpu.VMEM((mine, LANES, rows), f32),
            pltpu.VMEM((mine, terms, LANES, rows), f32),
            pltpu.SMEM((terms, taper_count * (taper_count + 1) // 2), f32),
            pltpu.VMEM((2, rows, LANES), f32),
            dma((2, half)), dma((2, half)),
            dma((2, half)), dma((2, half)),
            dma((2, half)), dma((2, half)),
            dma((half,)), dma((half,)),
            dma((mine, half)), dma((mine, half)),
            dma((mine, ITERS - 1, half)), dma((mine, ITERS - 1, half)),
            dma((mine,)), dma((mine,)),
            dma((mine,)), dma((mine,)),
        ],
        compiler_params=pltpu.CompilerParams(collective_id=0, has_side_effects=True),
    )(
        series.reshape(count, half, sub_rows, LANES),
        tapers.reshape(taper_count, half, sub_rows, LANES),
        concentration,
        qi_weights,
    )
    return (
        spectrum.reshape(count, 1, local_len),
        qi_terms.reshape(count, terms, 1, local_len),
    )


def solution(mesh):
    placed = (P("sa", "af"), P(None, "af"), P(), P())
    return jax.shard_map(
        functools.partial(local, mesh.shape["sa"]),
        mesh=mesh,
        in_specs=placed,
        out_specs=(P("sa", "af", None), P("sa", None, "af", None)),
        check_vma=False,
    )
```

time: 228 us -> 117 us (0.51)
  waiting for transfers between devices: 116 us -> 0 us
  Pallas kernels: 81 us -> 107 us
  starting transfers between devices: 14.3 us -> 0 us
  other arithmetic: 11.8 us -> 0 us
  local copies, waits for them, and re-layouts: 4.21 us -> 9.28 us
    all_to_all x2 -> x0, waiting for transfers between devices: 116 us -> none  [the longest x1 93.5 us: local(): recv = lax.all_to_all(turned, 'af', split_axis=0, concat_axis=0, tiled=True)]
    pallas_call x6 -> x1, Pallas kernels: 81 us -> 107 us  [local(): pl.pallas_call(functools.partial(fused_kernel, n, cores), out_shape=(jax....]
    all_to_all x2 -> x0, starting transfers between devices: 14.3 us -> none  [the longest x1 8.34 us: local(): got = lax.all_to_all(both, 'af', split_axis=0, concat_axis=0, tiled=True)]
    unnamed x4 -> x6, local copies, waits for them, and re-layouts: 1.54 us -> 9.28 us
    reduce_sum x5 -> x0, other arithmetic: 5.25 us -> none  [the longest x2 3.13 us: local(): sums = total_over_devices(jnp.sum(estimate, axis=1), shards, sweep)]
  transfers between devices with their start and end apart: 2 -> 0, of which waited for: 2 -> 0; matrix products, arithmetic and copies ran while one was open for 2% -> 0% of each run, Pallas kernels for 0% -> 0%
where the time goes in v1:
time: 117 us
  Pallas kernels  107 us (91%)
  local copies, waits for them, and re-layouts  9.28 us (8%)
    pallas_call x1, Pallas kernels, local(): pl.pallas_call(functools.partial(fused_kernel, n, cores), out_shape=(jax....  107 us
    unnamed x6, local copies, waits for them, and re-layouts  9.28 us

profile of v1, /device:TPU:0, one launch (start us, length us, event | category | flops | bytes accessed | tf_op | source)
XLA Modules:
  0.0 117.0 jit_solution(14514777293338062868)
XLA Ops:
  0.6 1.3 %copy.6.mix_ref = f32[4,10,10]{2,1,0:T(8,128)} copy(f32[4,10,10]{2,0,1:T(4,128)} %param.7) | data formatting | bytes 3200 | tf_op args[3]
  2.0 1.7 %copy.9 = f32[1,4,128,128]{3,2,1,0:T(8,128)} copy(f32[1,4,128,128]{3,1,2,0:T(4,128)} %bitcast.14) | data formatting | bytes 524288
  3.6 1.4 %copy.10 = f32[2,8,128,128]{3,2,1,0:T(8,128)S(1)} copy(f32[2,8,128,128]{3,1,2,0:T(8,128)} %bitcast.12) | data formatting | bytes 2097152
  5.1 0.9 slice
  6.0 107.0 %shard_map.59 = (f32[4,128,128]{2,1,0:T(8,128)}, f32[4,4,128,128]{3,2,1,0:T(8,128)}) custom-call(f32[4,8,16,128]{3,2,1,0:T(8,128)} %bitcast.11, f32[10,8,16,128]{3,2,1,0:T(8,128)} %bitcast.10, f32[10]{0:T(128)} %keep_ref.1, f32[4,10,10]{2,1,0:T(8,128)} %copy.6.mix_ref), custom_call_target="tpu_custom_call" | custom-call | tf_op jit(solution)/shard_map/pallas_call | solution.py:441
  113.0 1.7 %copy.13 = f32[4,1,16384]{2,1,0:T(1,128)} copy(f32[4,1,16384]{2,1,0:T(1,128)} %bitcast.15) | data formatting | bytes 524288
  114.7 2.3 %copy.14 = f32[4,4,1,16384]{3,2,1,0:T(1,128)} copy(f32[4,4,1,16384]{3,2,1,0:T(1,128)} %bitcast.13) | data formatting | bytes 2097152

commit v2 on v1

--- a/solution.py
+++ b/solution.py
@@ -95,22 +95,27 @@
 
 
 def fused_kernel(
-    n, cores, series_ref, tapers_ref, keep_ref, mix_ref, spec_ref, qi_ref,
-    ser, tap, zbuf, recv, en_out, en_in, sum_out, sum_in, left, right, inner, weigh,
+    n, cores, lead, series_ref, tapers_ref, keep_ref, mix_ref, spec_ref, qi_ref,
+    stage, ser_src, tap_src, ser, tap, zbuf, recv, en_out, en_in, sum_out, sum_in, left, right, inner, weigh,
     spec, power, est, qi, spec_out, qi_out, pairs, folded,
     ser_ss, ser_rs, tap_ss, tap_rs, core_ss, core_rs, en_ss, en_rs, z_ss, z_rs,
     sum_ss, sum_rs, qo_ss, qo_rs, so_ss, so_rs,
 ):
     half = n // 2
-    count, sub_rows = series_ref.shape[0], series_ref.shape[2]
+    count, sub_rows = ser_src.shape[0], ser_src.shape[2]
     mine = count // 2
-    tapers, terms = tap.shape[1], mix_ref.shape[0]
+    tapers, terms = tap.shape[1], mix_ref.shape[1]
     group = tapers // cores
+    sizes = (lead, group - lead)
+    starts = (0, lead)
+    places = (0, cores * lead)
+    order = [c * group + starts[b] + i for b in range(2) for c in range(cores) for i in range(sizes[b])]
     rows = half * sub_rows
     tall = spec.shape[2]
     extra = tall - rows
     local_len = rows * LANES
     length_all = local_len * n
+    tile = min(8, sub_rows)
     f32 = jnp.float32
     me, core = lax.axis_index("af"), lax.axis_index("sa")
     g, h = me // half, lax.rem(me, half)
@@ -136,41 +141,57 @@
     for dg, dh in peers:
         pl.semaphore_signal(barrier, inc=1, device_id={"af": flat(ahead(dg, dh))}, device_id_type=MESH)
     pl.semaphore_signal(barrier, inc=1, device_id={"sa": other_core}, device_id_type=MESH)
+
+    for j in range(rows):
+        lanes = slice(j * LANES, (j + 1) * LANES)
+        stage[0, 8 * j : 8 * j + 8] = tapers_ref[0:8, lanes]
+        stage[1, 8 * j : 8 * j + tapers - 8] = tapers_ref[8:tapers, lanes]
+        stage[1, 8 * j + tapers - 8 : 8 * j + tapers - 8 + count] = series_ref[:, lanes]
+    for row in range(tapers + count):
+        for j in range(rows // tile):
+            part = stage[row // 8, pl.ds(8 * j * tile + row % 8, tile, stride=8)]
+            at = (j * tile // sub_rows, slice(j * tile % sub_rows, j * tile % sub_rows + tile))
+            if row < tapers:
+                tap_src[row, at[0], at[1]] = part
+            else:
+                ser_src[row - tapers, at[0], at[1]] = part
     pl.semaphore_wait(barrier, n)
 
     def ser_copy(dg, dh):
         to = ahead(dg, dh)
         return remote(
-            series_ref.at[pl.ds(to[0] * mine, mine), to[1]], ser.at[me],
+            ser_src.at[pl.ds(to[0] * mine, mine), to[1]], ser.at[me],
             ser_ss.at[dg, dh], ser_rs.at[dg, dh], {"af": flat(to)},
         )
 
-    def tap_copy(dg, dh):
+    def tap_copy(b, dg, dh):
         to = ahead(dg, dh)
-        own = pl.ds(core * group, group)
         return remote(
-            tapers_ref.at[own, to[1]], tap.at[me, own],
-            tap_ss.at[dg, dh], tap_rs.at[dg, dh], {"af": flat(to)},
+            tap_src.at[pl.ds(core * group + starts[b], sizes[b]), to[1]],
+            tap.at[me, pl.ds(places[b] + core * sizes[b], sizes[b])],
+            tap_ss.at[b, dg, dh], tap_rs.at[b, dg, dh], {"af": flat(to)},
         )
 
-    def core_copy(dg, dh):
-        at = tap.at[flat(behind(dg, dh)), pl.ds(core * group, group)]
-        return remote(at, at, core_ss.at[dg, dh], core_rs.at[dg, dh], {"sa": other_core})
+    def core_copy(b, dg, dh):
+        at = tap.at[flat(behind(dg, dh)), pl.ds(places[b] + core * sizes[b], sizes[b])]
+        return remote(at, at, core_ss.at[b, dg, dh], core_rs.at[b, dg, dh], {"sa": other_core})
 
     for dg, dh in peers:
-        tap_copy(dg, dh).start()
         ser_copy(dg, dh).start()
+        tap_copy(0, dg, dh).start()
+    for dg, dh in peers:
+        tap_copy(1, dg, dh).start()
 
     for s in range(mine):
-        ser[me, s] = series_ref[g * mine + s, h]
-    for k in range(tapers):
-        tap[me, k] = tapers_ref[k, h]
+        ser[me, s] = ser_src[g * mine + s, h]
+    for i, k in enumerate(order):
+        tap[me, i] = tap_src[k, h]
     for t in range(terms):
         p = 0
         for j in range(tapers):
             for k in range(j, tapers):
-                value = mix_ref[t, j, k]
-                pairs[t, p] = value if j == k else value + mix_ref[t, k, j]
+                value = mix_ref[order[j], t, order[k]]
+                pairs[t, p] = value if j == k else value + mix_ref[order[k], t, order[j]]
                 p += 1
 
     def frequency(shape):
@@ -186,7 +207,6 @@
     first = jnp.where(upper, 1, 0) == g
     inside = at < rows
     once = at == rows
-    zero = jnp.zeros_like(c)
     take0 = jnp.where(single, jnp.where(inside | once, jnp.where(first, 1.0, 0.0), 0.0), jnp.where(inside, 1.0, 0.0))
     take1 = jnp.where(single, jnp.where(inside | once, jnp.where(first, 0.0, 1.0), 0.0), 0.0)
     plain = jnp.where(single, 0.0, jnp.where(inside, 1.0, 0.0))
@@ -219,45 +239,24 @@
     en_out[...] = jnp.zeros_like(en_out)
     sum_out[...] = jnp.zeros_like(sum_out)
 
-    for dg, dh in peers:
-        tap_copy(dg, dh).wait_recv()
-        core_copy(dg, dh).start()
-    for dg, dh in peers:
-        ser_copy(dg, dh).wait_recv()
-    for dg, dh in peers:
-        core_copy(dg, dh).wait_recv()
-
-    def energy(p, total):
-        one, two = tap[p, 0], tap[p, 1]
-        new = []
-        for s in range(mine):
-            a, b = ser[p, s] * one, ser[p, s] * two
-            new.append(total[s] + (a * a + b * b))
-        return tuple(new)
-
-    total = lax.fori_loop(0, n, energy, tuple(jnp.zeros((sub_rows, LANES), f32) for _ in range(mine)))
-    for s in range(mine):
-        en_out[s : s + 1] = jnp.sum(total[s], axis=0, keepdims=True)
-
-    def en_copy(dh):
-        return remote(en_out, en_in.at[dh], en_ss.at[dh], en_rs.at[dh], friend(dh))
-
-    for dh in range(1, half):
-        en_copy(dh).start()
-
-    def z_copy(s, dh):
-        to = lax.rem(h + dh, half)
-        return remote(
-            zbuf.at[to, s], recv.at[s, :, :, h], z_ss.at[s, dh], z_rs.at[s, dh], friend(dh)
-        )
+    def arrive(b):
+        for dg, dh in peers:
+            tap_copy(b, dg, dh).wait_recv()
+            core_copy(b, dg, dh).start()
+        if b == 0:
+            for dg, dh in peers:
+                ser_copy(dg, dh).wait_recv()
+        for dg, dh in peers:
+            core_copy(b, dg, dh).wait_recv()
 
     sign = (1 - 2 * g).astype(f32)
-    tile = min(8, sub_rows)
-    for s in range(mine):
+
+    def front(s, b):
+        lo, hi = places[b], places[b] + cores * sizes[b]
         for i in range(sub_rows // tile):
             part = pl.ds(i * tile, tile)
 
-            def front(k, carry, s=s, part=part):
+            def body(k, carry):
                 got = []
                 for p in range(n):
                     value = ser[p, s, part] * tap[p, k, part]
@@ -269,12 +268,48 @@
                     zbuf[u, s, k, 1, part] = out[half][0] if u == 0 else im
                 return carry
 
-            lax.fori_loop(0, tapers, front, 0)
-        for dh in range(1, half):
-            z_copy(s, dh).start()
-        for k in range(tapers):
+            lax.fori_loop(lo, hi, body, 0)
+        for k in range(lo, hi):
             for part in range(2):
                 recv[s, k, part, h] = zbuf[h, s, k, part]
+
+    def z_copy(s, b, dh):
+        to = lax.rem(h + dh, half)
+        at = pl.ds(places[b], cores * sizes[b])
+        return remote(
+            zbuf.at[to, s, at], recv.at[s, at, :, h], z_ss.at[s, b, dh], z_rs.at[s, b, dh], friend(dh)
+        )
+
+    def z_start(s, b):
+        for dh in range(1, half):
+            z_copy(s, b, dh).start()
+
+    def en_copy(dh):
+        return remote(en_out, en_in.at[dh], en_ss.at[dh], en_rs.at[dh], friend(dh))
+
+    def energy(p, total):
+        one, two = tap[p, 0], tap[p, 1]
+        new = []
+        for s in range(mine):
+            a, b = ser[p, s] * one, ser[p, s] * two
+            new.append(total[s] + (a * a + b * b))
+        return tuple(new)
+
+    arrive(0)
+    front(0, 0)
+    z_start(0, 0)
+    total = lax.fori_loop(0, n, energy, tuple(jnp.zeros((sub_rows, LANES), f32) for _ in range(mine)))
+    for s in range(mine):
+        en_out[s : s + 1] = jnp.sum(total[s], axis=0, keepdims=True)
+    for dh in range(1, half):
+        en_copy(dh).start()
+    arrive(1)
+    front(0, 1)
+    z_start(0, 1)
+    for s in range(1, mine):
+        for b in range(2):
+            front(s, b)
+        z_start(s, 0)
 
     for dh in range(1, half):
         en_copy(dh).wait_recv()
@@ -282,24 +317,23 @@
     for dh in range(1, half):
         total += en_in[dh]
     variance0 = [jnp.sum(total[s : s + 1]) * (0.5 / length_all) for s in range(mine)]
-    keep = [keep_ref[k] for k in range(tapers)]
-
-    def sum_copy(s, it, dh):
-        return remote(
-            sum_out.at[s, it], sum_in.at[s, it, dh], sum_ss.at[s, it, dh], sum_rs.at[s, it, dh], friend(dh)
-        )
-
-    def share(s, it, total):
-        sum_out[s, it, 0:1] = jnp.sum(total, axis=0, keepdims=True)
+    keep = [keep_ref[k] for k in order]
+
+    def sum_copy(it, dh):
+        return remote(sum_out.at[it], sum_in.at[it, dh], sum_ss.at[it, dh], sum_rs.at[it, dh], friend(dh))
+
+    def share(it, totals):
+        for s, total in enumerate(totals):
+            sum_out[it, s : s + 1] = jnp.sum(total, axis=0, keepdims=True)
         for dh in range(1, half):
-            sum_copy(s, it, dh).start()
-
-    def collect(s, it):
-        total = sum_out[s, it]
+            sum_copy(it, dh).start()
+
+    def collect(it):
+        total = sum_out[it]
         for dh in range(1, half):
-            sum_copy(s, it, dh).wait_recv()
-            total += sum_in[s, it, dh]
-        return jnp.sum(total) / length_all
+            sum_copy(it, dh).wait_recv()
+            total += sum_in[it, dh]
+        return [jnp.sum(total[s : s + 1]) / length_all for s in range(mine)]
 
     def transform(s):
         def body(kk, carry):
@@ -376,52 +410,65 @@
 
         return folded[0].T, folded[1].T
 
-    def qi_copy(s):
-        return remote(qi_out.at[s], qi_ref.at[g * mine + s], qo_ss.at[s], qo_rs.at[s], partner)
+    def qi_copy(s, t):
+        return remote(qi_out.at[s, t], qi_ref.at[g * mine + s, t], qo_ss.at[s, t], qo_rs.at[s, t], partner)
 
     def spec_copy(s):
         return remote(spec_out.at[s], spec_ref.at[g * mine + s], so_ss.at[s], so_rs.at[s], partner)
 
-    def outputs_qi(s):
-        for t in range(terms):
+    def outputs_qi(s, which):
+        for t in which:
             own, sent = assemble(qi.at[s, t])
             qi_ref[g * mine + s, t] = own
             qi_out[s, t] = sent
-        qi_copy(s).start()
-
-    def outputs_spec(s):
+            qi_copy(s, t).start()
+
+    totals = []
+    for s in range(mine):
+        for b in range(2):
+            for dh in range(1, half):
+                z_copy(s, b, dh).wait_recv()
+        transform(s)
+        totals.append(combine(s, variance0[s]))
+        if s < mine - 1:
+            outputs_qi(s, range(terms))
+            z_start(s + 1, 1)
+    for it in range(1, ITERS):
+        share(it - 1, totals)
+        outputs_qi(mine - 1, range(terms * (it - 1) // (ITERS - 1), terms * it // (ITERS - 1)))
+        variance = collect(it - 1)
+        totals = [sweep(s, variance[s]) for s in range(mine)]
+    for s in range(mine):
         own, sent = assemble(est.at[s])
         spec_ref[g * mine + s] = own
         spec_out[s] = sent
         spec_copy(s).start()
 
     for s in range(mine):
-        for dh in range(1, half):
-            z_copy(s, dh).wait_recv()
-        transform(s)
-        share(s, 0, combine(s, variance0[s]))
-        outputs_qi(s)
-        for it in range(1, ITERS):
-            total = sweep(s, collect(s, it - 1))
-            if it < ITERS - 1:
-                share(s, it, total)
-        outputs_spec(s)
-
+        for t in range(terms):
+            qi_copy(s, t).wait_recv()
+        spec_copy(s).wait_recv()
     for s in range(mine):
-        qi_copy(s).wait_recv()
-        spec_copy(s).wait_recv()
-        qi_copy(s).wait_send()
+        for t in range(terms):
+            qi_copy(s, t).wait_send()
         spec_copy(s).wait_send()
         for dh in range(1, half):
-            z_copy(s, dh).wait_send()
-            for it in range(ITERS - 1):
-                sum_copy(s, it, dh).wait_send()
+            for b in range(2):
+                z_copy(s, b, dh).wait_send()
     for dh in range(1, half):
         en_copy(dh).wait_send()
+        for it in range(ITERS - 1):
+            sum_copy(it, dh).wait_send()
     for dg, dh in peers:
-        tap_copy(dg, dh).wait_send()
         ser_copy(dg, dh).wait_send()
-        core_copy(dg, dh).wait_send()
+        for b in range(2):
+            tap_copy(b, dg, dh).wait_send()
+            core_copy(b, dg, dh).wait_send()
+
+
+def hand_kernel(spec_ref, qi_ref, spec_out, qi_out):
+    spec_out[...] = spec_ref[...]
+    qi_out[...] = qi_ref[...]
 
 
 def local(cores, series, tapers, concentration, qi_weights):
@@ -433,28 +480,33 @@
     sub_rows = local_len // (half * LANES)
     rows = local_len // LANES
     tall = rows + CHUNK
+    lead = (taper_count // cores + 1) // 2
     f32 = jnp.float32
     bf16 = jnp.bfloat16
     vmem = pl.BlockSpec(memory_space=pltpu.VMEM)
     smem = pl.BlockSpec(memory_space=pltpu.SMEM)
     dma = pltpu.SemaphoreType.DMA
-    spectrum, qi_terms = pl.pallas_call(
-        functools.partial(fused_kernel, n, cores),
-        out_shape=(
-            jax.ShapeDtypeStruct((count, LANES, rows), f32),
-            jax.ShapeDtypeStruct((count, terms, LANES, rows), f32),
-        ),
+    shapes = (
+        jax.ShapeDtypeStruct((count, LANES, rows), f32),
+        jax.ShapeDtypeStruct((count, terms, LANES, rows), f32),
+    )
+    outs = pl.pallas_call(
+        functools.partial(fused_kernel, n, cores, lead),
+        out_shape=shapes,
         in_specs=[vmem, vmem, smem, smem],
         out_specs=(vmem, vmem),
         scratch_shapes=[
+            pltpu.VMEM((2, 8 * rows, LANES), f32),
+            pltpu.VMEM((count, half, sub_rows, LANES), f32),
+            pltpu.VMEM((taper_count, half, sub_rows, LANES), f32),
             pltpu.VMEM((n, mine, sub_rows, LANES), f32),
             pltpu.VMEM((n, taper_count, sub_rows, LANES), f32),
             pltpu.VMEM((half, mine, taper_count, 2, sub_rows, LANES), f32),
             pltpu.VMEM((mine, taper_count, 2, half, sub_rows, LANES), f32),
             pltpu.VMEM((8, LANES), f32),
             pltpu.VMEM((half, 8, LANES), f32),
-            pltpu.VMEM((mine, ITERS - 1, 8, LANES), f32),
-            pltpu.VMEM((mine, ITERS - 1, half, 8, LANES), f32),
+            pltpu.VMEM((ITERS - 1, 8, LANES), f32),
+            pltpu.VMEM((ITERS - 1, half, 8, LANES), f32),
             pltpu.VMEM((2, rows + tall, 2 * rows), bf16),
             pltpu.VMEM((2, 2 * LANES, 2 * LANES), bf16),
             pltpu.VMEM((2, tall, LANES), f32),
@@ -468,21 +520,19 @@
             pltpu.SMEM((terms, taper_count * (taper_count + 1) // 2), f32),
             pltpu.VMEM((2, rows, LANES), f32),
             dma((2, half)), dma((2, half)),
-            dma((2, half)), dma((2, half)),
-            dma((2, half)), dma((2, half)),
+            dma((2, 2, half)), dma((2, 2, half)),
+            dma((2, 2, half)), dma((2, 2, half)),
             dma((half,)), dma((half,)),
-            dma((mine, half)), dma((mine, half)),
-            dma((mine, ITERS - 1, half)), dma((mine, ITERS - 1, half)),
-            dma((mine,)), dma((mine,)),
+            dma((mine, 2, half)), dma((mine, 2, half)),
+            dma((ITERS - 1, half)), dma((ITERS - 1, half)),
+            dma((mine, terms)), dma((mine, terms)),
             dma((mine,)), dma((mine,)),
         ],
         compiler_params=pltpu.CompilerParams(collective_id=0, has_side_effects=True),
-    )(
-        series.reshape(count, half, sub_rows, LANES),
-        tapers.reshape(taper_count, half, sub_rows, LANES),
-        concentration,
-        qi_weights,
-    )
+    )(series, tapers, concentration, qi_weights.transpose(1, 0, 2))
+    spectrum, qi_terms = pl.pallas_call(
+        hand_kernel, out_shape=shapes, in_specs=[vmem, vmem], out_specs=(vmem, vmem)
+    )(*outs)
     return (
         spectrum.reshape(count, 1, local_len),
         qi_terms.reshape(count, terms, 1, local_len),

time: 117 us -> 98.5 us (0.84)
  Pallas kernels: 107 us -> 97.6 us
  local copies, waits for them, and re-layouts: 9.28 us -> 0 us
    pallas_call x1 -> x2, Pallas kernels: 107 us -> 97.6 us  [the longest x1 95.3 us: local(): pl.pallas_call(functools.partial(fused_kernel, n, cores, lead), out_shape...]
    unnamed x6 -> x0, local copies, waits for them, and re-layouts: 9.28 us -> none
where the time goes in v2:
time: 98.5 us; the launch traced here: 98.3 us
  Pallas kernels  97.6 us (99%)
    pallas_call x1, Pallas kernels, local(): pl.pallas_call(functools.partial(fused_kernel, n, cores, lead), out_shape...  95.3 us
    pallas_call x1, Pallas kernels, local(): pl.pallas_call(hand_kernel, out_shape=shapes, in_specs=[vmem, vmem], out_...  2.39 us

profile of v2, /device:TPU:0, one launch (start us, length us, event | category | flops | bytes accessed | tf_op | source)
XLA Modules:
  0.0 98.3 jit_solution(12328244069720536925)
XLA Ops:
  0.6 95.3 %shard_map.59 = (f32[4,128,128]{2,1,0:T(8,128)}, f32[4,4,128,128]{3,2,1,0:T(8,128)}) custom-call(f32[4,16384]{1,0:T(4,128)} %series_ref.1, f32[10,16384]{1,0:T(8,128)} %tapers_ref.1, f32[10]{0:T(128)} %keep_ref.1, f32[10,4,10]{2,1,0:T(4,128)} %bitcast.3), custom_call_target="tpu_custom_call" | custom-call | tf_op jit(solution)/shard_map/pallas_call | solution.py:493
  95.9 2.4 %shard_map.60 = (f32[4,128,128]{2,1,0:T(8,128)}, f32[4,4,128,128]{3,2,1,0:T(8,128)}) custom-call(f32[4,128,128]{2,1,0:T(8,128)} %get-tuple-element.6.spec_ref, f32[4,4,128,128]{3,2,1,0:T(8,128)} %get-tuple-element.7.qi_ref), custom_call_target="tpu_custom_call" | custom-call | tf_op jit(solution)/shard_map/pallas_call | solution.py:533

commit v3 on v2

--- a/solution.py
+++ b/solution.py
@@ -95,21 +95,28 @@
 
 
 def fused_kernel(
-    n, cores, lead, series_ref, tapers_ref, keep_ref, mix_ref, spec_ref, qi_ref,
-    stage, ser_src, tap_src, ser, tap, zbuf, recv, en_out, en_in, sum_out, sum_in, left, right, inner, weigh,
+    n, cores, sizes, series_hbm, tapers_hbm, keep_ref, mix_ref, spec_ref, qi_ref,
+    series_ref, tapers_ref, stage, ser_src, tap_src, ser, tap, zbuf, recv, en_out, en_in, sum_out, sum_in, left, right, inner, weigh,
     spec, power, est, qi, spec_out, qi_out, pairs, folded,
     ser_ss, ser_rs, tap_ss, tap_rs, core_ss, core_rs, en_ss, en_rs, z_ss, z_rs,
-    sum_ss, sum_rs, qo_ss, qo_rs, so_ss, so_rs,
+    sum_ss, sum_rs, qo_ss, qo_rs, so_ss, so_rs, in_sem,
 ):
+    inputs = [
+        pltpu.make_async_copy(series_hbm, series_ref, in_sem.at[0]),
+        pltpu.make_async_copy(tapers_hbm, tapers_ref, in_sem.at[1]),
+    ]
+    for copy in inputs:
+        copy.start()
     half = n // 2
     count, sub_rows = ser_src.shape[0], ser_src.shape[2]
     mine = count // 2
     tapers, terms = tap.shape[1], mix_ref.shape[1]
     group = tapers // cores
-    sizes = (lead, group - lead)
-    starts = (0, lead)
-    places = (0, cores * lead)
-    order = [c * group + starts[b] + i for b in range(2) for c in range(cores) for i in range(sizes[b])]
+    batches = range(len(sizes))
+    starts = [sum(sizes[:b]) for b in batches]
+    places = [cores * start for start in starts]
+    order = [c * group + starts[b] + i for b in batches for c in range(cores) for i in range(sizes[b])]
+    early = [order.index(0), order.index(1)]
     rows = half * sub_rows
     tall = spec.shape[2]
     extra = tall - rows
@@ -119,14 +126,11 @@
     f32 = jnp.float32
     me, core = lax.axis_index("af"), lax.axis_index("sa")
     g, h = me // half, lax.rem(me, half)
-    peers = [(dg, dh) for dg in (1, 0) for dh in range(half) if dg or dh]
+    peers = [(dg, dh) for dg in (0, 1) for dh in range(half) if dg or dh]
     single = h == 0
 
     def ahead(dg, dh):
         return lax.rem(g + dg, 2), lax.rem(h + dh, half)
-
-    def behind(dg, dh):
-        return lax.rem(g + dg, 2), lax.rem(h + half - dh, half)
 
     def flat(at):
         return at[0] * half + at[1]
@@ -142,6 +146,8 @@
         pl.semaphore_signal(barrier, inc=1, device_id={"af": flat(ahead(dg, dh))}, device_id_type=MESH)
     pl.semaphore_signal(barrier, inc=1, device_id={"sa": other_core}, device_id_type=MESH)
 
+    for copy in inputs:
+        copy.wait()
     for j in range(rows):
         lanes = slice(j * LANES, (j + 1) * LANES)
         stage[0, 8 * j : 8 * j + 8] = tapers_ref[0:8, lanes]
@@ -161,7 +167,7 @@
         to = ahead(dg, dh)
         return remote(
             ser_src.at[pl.ds(to[0] * mine, mine), to[1]], ser.at[me],
-            ser_ss.at[dg, dh], ser_rs.at[dg, dh], {"af": flat(to)},
+            ser_ss.at[0], ser_rs.at[0], {"af": flat(to)},
         )
 
     def tap_copy(b, dg, dh):
@@ -169,23 +175,36 @@
         return remote(
             tap_src.at[pl.ds(core * group + starts[b], sizes[b]), to[1]],
             tap.at[me, pl.ds(places[b] + core * sizes[b], sizes[b])],
-            tap_ss.at[b, dg, dh], tap_rs.at[b, dg, dh], {"af": flat(to)},
+            tap_ss.at[b], tap_rs.at[b], {"af": flat(to)},
         )
 
-    def core_copy(b, dg, dh):
-        at = tap.at[flat(behind(dg, dh)), pl.ds(places[b] + core * sizes[b], sizes[b])]
-        return remote(at, at, core_ss.at[b, dg, dh], core_rs.at[b, dg, dh], {"sa": other_core})
-
-    for dg, dh in peers:
-        ser_copy(dg, dh).start()
-        tap_copy(0, dg, dh).start()
-    for dg, dh in peers:
-        tap_copy(1, dg, dh).start()
+    def core_copy(b):
+        at = tap.at[:, pl.ds(places[b] + core * sizes[b], sizes[b])]
+        return remote(at, at, core_ss.at[b], core_rs.at[b], {"sa": other_core})
+
+    def settle(like, semaphore):
+        pltpu.make_async_copy(like, like, semaphore).wait()
+
+    ser_like = ser.at[pl.ds(0, n - 1)]
+    tap_like = [tap.at[pl.ds(0, n - 1), pl.ds(places[b], sizes[b])] for b in batches]
+    z_like = [
+        [recv.at[s, pl.ds(places[b], cores * sizes[b]), :, pl.ds(0, half - 1)] for b in batches]
+        for s in range(mine)
+    ]
+    en_like = en_in.at[pl.ds(1, half - 1)]
+    sum_like = [sum_in.at[it, pl.ds(1, half - 1)] for it in range(ITERS - 1)]
+
+    for b in batches:
+        for dg, dh in peers:
+            if b == 0:
+                ser_copy(dg, dh).start()
+            tap_copy(b, dg, dh).start()
 
     for s in range(mine):
         ser[me, s] = ser_src[g * mine + s, h]
-    for i, k in enumerate(order):
-        tap[me, i] = tap_src[k, h]
+    for b in batches:
+        for i in range(sizes[b]):
+            tap[me, places[b] + core * sizes[b] + i] = tap_src[core * group + starts[b] + i, h]
     for t in range(terms):
         p = 0
         for j in range(tapers):
@@ -240,14 +259,11 @@
     sum_out[...] = jnp.zeros_like(sum_out)
 
     def arrive(b):
-        for dg, dh in peers:
-            tap_copy(b, dg, dh).wait_recv()
-            core_copy(b, dg, dh).start()
+        settle(tap_like[b], tap_rs.at[b])
+        core_copy(b).start()
         if b == 0:
-            for dg, dh in peers:
-                ser_copy(dg, dh).wait_recv()
-        for dg, dh in peers:
-            core_copy(b, dg, dh).wait_recv()
+            settle(ser_like, ser_rs.at[0])
+        core_copy(b).wait_recv()
 
     sign = (1 - 2 * g).astype(f32)
 
@@ -277,7 +293,7 @@
         to = lax.rem(h + dh, half)
         at = pl.ds(places[b], cores * sizes[b])
         return remote(
-            zbuf.at[to, s, at], recv.at[s, at, :, h], z_ss.at[s, b, dh], z_rs.at[s, b, dh], friend(dh)
+            zbuf.at[to, s, at], recv.at[s, at, :, h], z_ss.at[s, b], z_rs.at[s, b], friend(dh)
         )
 
     def z_start(s, b):
@@ -285,42 +301,48 @@
             z_copy(s, b, dh).start()
 
     def en_copy(dh):
-        return remote(en_out, en_in.at[dh], en_ss.at[dh], en_rs.at[dh], friend(dh))
+        return remote(en_out, en_in.at[dh], en_ss.at[0], en_rs.at[0], friend(dh))
 
     def energy(p, total):
-        one, two = tap[p, 0], tap[p, 1]
+        one, two = tap[p, early[0]], tap[p, early[1]]
         new = []
         for s in range(mine):
             a, b = ser[p, s] * one, ser[p, s] * two
             new.append(total[s] + (a * a + b * b))
         return tuple(new)
 
-    arrive(0)
-    front(0, 0)
-    z_start(0, 0)
-    total = lax.fori_loop(0, n, energy, tuple(jnp.zeros((sub_rows, LANES), f32) for _ in range(mine)))
-    for s in range(mine):
-        en_out[s : s + 1] = jnp.sum(total[s], axis=0, keepdims=True)
-    for dh in range(1, half):
-        en_copy(dh).start()
-    arrive(1)
-    front(0, 1)
-    z_start(0, 1)
+    for b in batches:
+        arrive(b)
+        front(0, b)
+        z_start(0, b)
+        if max(early) < places[b] + cores * sizes[b] and max(early) >= places[b]:
+            total = lax.fori_loop(0, n, energy, tuple(jnp.zeros((sub_rows, LANES), f32) for _ in range(mine)))
+            for s in range(mine):
+                en_out[s : s + 1] = jnp.sum(total[s], axis=0, keepdims=True)
+            for dh in range(1, half):
+                en_copy(dh).start()
     for s in range(1, mine):
-        for b in range(2):
+        for b in batches:
             front(s, b)
-        z_start(s, 0)
-
-    for dh in range(1, half):
-        en_copy(dh).wait_recv()
-    total = en_out[...]
-    for dh in range(1, half):
-        total += en_in[dh]
-    variance0 = [jnp.sum(total[s : s + 1]) * (0.5 / length_all) for s in range(mine)]
+            z_start(s, b)
+
+    settle(ser_like, ser_ss.at[0])
+    for b in batches:
+        settle(tap_like[b], tap_ss.at[b])
+        core_copy(b).wait_send()
+
+    def first_variance():
+        settle(en_like, en_rs.at[0])
+        settle(en_like, en_ss.at[0])
+        total = en_out[...]
+        for dh in range(1, half):
+            total += en_in[dh]
+        return [jnp.sum(total[s : s + 1]) * (0.5 / length_all) for s in range(mine)]
+
     keep = [keep_ref[k] for k in order]
 
     def sum_copy(it, dh):
-        return remote(sum_out.at[it], sum_in.at[it, dh], sum_ss.at[it, dh], sum_rs.at[it, dh], friend(dh))
+        return remote(sum_out.at[it], sum_in.at[it, dh], sum_ss.at[it], sum_rs.at[it], friend(dh))
 
     def share(it, totals):
         for s, total in enumerate(totals):
@@ -329,13 +351,13 @@
             sum_copy(it, dh).start()
 
     def collect(it):
+        settle(sum_like[it], sum_rs.at[it])
         total = sum_out[it]
         for dh in range(1, half):
-            sum_copy(it, dh).wait_recv()
             total += sum_in[it, dh]
         return [jnp.sum(total[s : s + 1]) / length_all for s in range(mine)]
 
-    def transform(s):
+    def transform(s, b):
         def body(kk, carry):
             k = 2 * kk
             x = jnp.concatenate(
@@ -356,7 +378,7 @@
                 spec[1, k + i] = block[:, LANES:]
             return carry
 
-        lax.fori_loop(0, tapers // 2, body, 0)
+        lax.fori_loop(places[b] // 2, (places[b] + cores * sizes[b]) // 2, body, 0)
 
     def combine(s, variance):
         def body(i, total):
@@ -377,7 +399,7 @@
                     pair += 1
             for t in range(terms):
                 qi[s, t, at] = sums[t]
-            new = refine(0.5 * (powers[0] + powers[1]), powers, keep, variance)
+            new = refine(0.5 * (powers[early[0]] + powers[early[1]]), powers, keep, variance)
             est[s, at] = new
             return total + new * weigh[at]
 
@@ -411,10 +433,10 @@
         return folded[0].T, folded[1].T
 
     def qi_copy(s, t):
-        return remote(qi_out.at[s, t], qi_ref.at[g * mine + s, t], qo_ss.at[s, t], qo_rs.at[s, t], partner)
+        return remote(qi_out.at[s, t], qi_ref.at[g * mine + s, t], qo_ss.at[s], qo_rs.at[s], partner)
 
     def spec_copy(s):
-        return remote(spec_out.at[s], spec_ref.at[g * mine + s], so_ss.at[s], so_rs.at[s], partner)
+        return remote(spec_out.at[s], spec_ref.at[g * mine + s], so_ss.at[0], so_rs.at[0], partner)
 
     def outputs_qi(s, which):
         for t in which:
@@ -425,14 +447,14 @@
 
     totals = []
     for s in range(mine):
-        for b in range(2):
-            for dh in range(1, half):
-                z_copy(s, b, dh).wait_recv()
-        transform(s)
+        for b in batches:
+            settle(z_like[s][b], z_rs.at[s, b])
+            transform(s, b)
+        if s == 0:
+            variance0 = first_variance()
         totals.append(combine(s, variance0[s]))
         if s < mine - 1:
             outputs_qi(s, range(terms))
-            z_start(s + 1, 1)
     for it in range(1, ITERS):
         share(it - 1, totals)
         outputs_qi(mine - 1, range(terms * (it - 1) // (ITERS - 1), terms * it // (ITERS - 1)))
@@ -445,25 +467,15 @@
         spec_copy(s).start()
 
     for s in range(mine):
-        for t in range(terms):
-            qi_copy(s, t).wait_recv()
-        spec_copy(s).wait_recv()
+        for b in batches:
+            settle(z_like[s][b], z_ss.at[s, b])
+    for it in range(ITERS - 1):
+        settle(sum_like[it], sum_ss.at[it])
     for s in range(mine):
-        for t in range(terms):
-            qi_copy(s, t).wait_send()
-        spec_copy(s).wait_send()
-        for dh in range(1, half):
-            for b in range(2):
-                z_copy(s, b, dh).wait_send()
-    for dh in range(1, half):
-        en_copy(dh).wait_send()
-        for it in range(ITERS - 1):
-            sum_copy(it, dh).wait_send()
-    for dg, dh in peers:
-        ser_copy(dg, dh).wait_send()
-        for b in range(2):
-            tap_copy(b, dg, dh).wait_send()
-            core_copy(b, dg, dh).wait_send()
+        settle(qi_out.at[s], qo_rs.at[s])
+        settle(qi_out.at[s], qo_ss.at[s])
+    settle(spec_out, so_rs.at[0])
+    settle(spec_out, so_ss.at[0])
 
 
 def hand_kernel(spec_ref, qi_ref, spec_out, qi_out):
@@ -480,22 +492,25 @@
     sub_rows = local_len // (half * LANES)
     rows = local_len // LANES
     tall = rows + CHUNK
-    lead = (taper_count // cores + 1) // 2
+    sizes = (1,) * (taper_count // cores)
     f32 = jnp.float32
     bf16 = jnp.bfloat16
     vmem = pl.BlockSpec(memory_space=pltpu.VMEM)
     smem = pl.BlockSpec(memory_space=pltpu.SMEM)
+    hbm = pl.BlockSpec(memory_space=pltpu.HBM)
     dma = pltpu.SemaphoreType.DMA
     shapes = (
         jax.ShapeDtypeStruct((count, LANES, rows), f32),
         jax.ShapeDtypeStruct((count, terms, LANES, rows), f32),
     )
     outs = pl.pallas_call(
-        functools.partial(fused_kernel, n, cores, lead),
+        functools.partial(fused_kernel, n, cores, sizes),
         out_shape=shapes,
-        in_specs=[vmem, vmem, smem, smem],
+        in_specs=[hbm, hbm, smem, smem],
         out_specs=(vmem, vmem),
         scratch_shapes=[
+            pltpu.VMEM(series.shape, f32),
+            pltpu.VMEM(tapers.shape, f32),
             pltpu.VMEM((2, 8 * rows, LANES), f32),
             pltpu.VMEM((count, half, sub_rows, LANES), f32),
             pltpu.VMEM((taper_count, half, sub_rows, LANES), f32),
@@ -519,14 +534,15 @@
             pltpu.VMEM((mine, terms, LANES, rows), f32),
             pltpu.SMEM((terms, taper_count * (taper_count + 1) // 2), f32),
             pltpu.VMEM((2, rows, LANES), f32),
-            dma((2, half)), dma((2, half)),
-            dma((2, 2, half)), dma((2, 2, half)),
-            dma((2, 2, half)), dma((2, 2, half)),
-            dma((half,)), dma((half,)),
-            dma((mine, 2, half)), dma((mine, 2, half)),
-            dma((ITERS - 1, half)), dma((ITERS - 1, half)),
-            dma((mine, terms)), dma((mine, terms)),
+            dma((1,)), dma((1,)),
+            dma((len(sizes),)), dma((len(sizes),)),
+            dma((len(sizes),)), dma((len(sizes),)),
+            dma((1,)), dma((1,)),
+            dma((mine, len(sizes))), dma((mine, len(sizes))),
+            dma((ITERS - 1,)), dma((ITERS - 1,)),
             dma((mine,)), dma((mine,)),
+            dma((1,)), dma((1,)),
+            dma((2,)),
         ],
         compiler_params=pltpu.CompilerParams(collective_id=0, has_side_effects=True),
     )(series, tapers, concentration, qi_weights.transpose(1, 0, 2))

time: 98.5 us -> 86.3 us (0.88)
  Pallas kernels: 97.6 us -> 85.4 us
    pallas_call x1, Pallas kernels: 95.3 us -> 83 us  [local(): pl.pallas_call(functools.partial(fused_kernel, n, cores, sizes), out_shap...]
where the time goes in v3:
time: 86.3 us; the launch traced here: 86 us
  Pallas kernels  85.4 us (99%)
    pallas_call x1, Pallas kernels, local(): pl.pallas_call(functools.partial(fused_kernel, n, cores, sizes), out_shap...  83 us
    pallas_call x1, Pallas kernels, local(): pl.pallas_call(hand_kernel, out_shape=shapes, in_specs=[vmem, vmem], out_...  2.39 us

profile of v3, /device:TPU:0, one launch (start us, length us, event | category | flops | bytes accessed | tf_op | source)
XLA Modules:
  0.0 86.0 jit_solution(15006066543097321816)
XLA Ops:
  0.6 83.0 %shard_map.59 = (f32[4,128,128]{2,1,0:T(8,128)}, f32[4,4,128,128]{3,2,1,0:T(8,128)}) custom-call(f32[4,16384]{1,0:T(4,128)} %series_hbm.1, f32[10,16384]{1,0:T(8,128)} %tapers_hbm.1, f32[10]{0:T(128)} %keep_ref.1, f32[10,4,10]{2,1,0:T(4,128)} %bitcast.3), custom_call_target="tpu_custom_call" | custom-call | tf_op jit(solution)/shard_map/pallas_call | solution.py:506
  83.6 2.4 %shard_map.60 = (f32[4,128,128]{2,1,0:T(8,128)}, f32[4,4,128,128]{3,2,1,0:T(8,128)}) custom-call(f32[4,128,128]{2,1,0:T(8,128)} %get-tuple-element.6.spec_ref, f32[4,4,128,128]{3,2,1,0:T(8,128)} %get-tuple-element.7.qi_ref), custom_call_target="tpu_custom_call" | custom-call | tf_op jit(solution)/shard_map/pallas_call | solution.py:549

commit v4 on v3

--- a/solution.py
+++ b/solution.py
@@ -97,9 +97,9 @@
 def fused_kernel(
     n, cores, sizes, series_hbm, tapers_hbm, keep_ref, mix_ref, spec_ref, qi_ref,
     series_ref, tapers_ref, stage, ser_src, tap_src, ser, tap, zbuf, recv, en_out, en_in, sum_out, sum_in, left, right, inner, weigh,
-    spec, power, est, qi, spec_out, qi_out, pairs, folded,
+    spec, power, est, qi, spec_out, qi_out, spec_own, qi_own, pairs, folded,
     ser_ss, ser_rs, tap_ss, tap_rs, core_ss, core_rs, en_ss, en_rs, z_ss, z_rs,
-    sum_ss, sum_rs, qo_ss, qo_rs, so_ss, so_rs, in_sem,
+    sum_ss, sum_rs, qo_ss, qo_rs, so_ss, so_rs, in_sem, own_sem,
 ):
     inputs = [
         pltpu.make_async_copy(series_hbm, series_ref, in_sem.at[0]),
@@ -163,11 +163,10 @@
                 ser_src[row - tapers, at[0], at[1]] = part
     pl.semaphore_wait(barrier, n)
 
-    def ser_copy(dg, dh):
+    def ser_copy(s, dg, dh):
         to = ahead(dg, dh)
         return remote(
-            ser_src.at[pl.ds(to[0] * mine, mine), to[1]], ser.at[me],
-            ser_ss.at[0], ser_rs.at[0], {"af": flat(to)},
+            ser_src.at[to[0] * mine + s, to[1]], ser.at[s, me], ser_ss.at[s], ser_rs.at[s], {"af": flat(to)}
         )
 
     def tap_copy(b, dg, dh):
@@ -185,7 +184,8 @@
     def settle(like, semaphore):
         pltpu.make_async_copy(like, like, semaphore).wait()
 
-    ser_like = ser.at[pl.ds(0, n - 1)]
+    ser_like = [ser.at[s, pl.ds(0, n - 1)] for s in range(mine)]
+    carried = [[s for s in range(mine) if (0 if s == 0 else len(sizes) - 1) == b] for b in batches]
     tap_like = [tap.at[pl.ds(0, n - 1), pl.ds(places[b], sizes[b])] for b in batches]
     z_like = [
         [recv.at[s, pl.ds(places[b], cores * sizes[b]), :, pl.ds(0, half - 1)] for b in batches]
@@ -196,12 +196,12 @@
 
     for b in batches:
         for dg, dh in peers:
-            if b == 0:
-                ser_copy(dg, dh).start()
+            for s in carried[b]:
+                ser_copy(s, dg, dh).start()
             tap_copy(b, dg, dh).start()
 
     for s in range(mine):
-        ser[me, s] = ser_src[g * mine + s, h]
+        ser[s, me] = ser_src[g * mine + s, h]
     for b in batches:
         for i in range(sizes[b]):
             tap[me, places[b] + core * sizes[b] + i] = tap_src[core * group + starts[b] + i, h]
@@ -261,8 +261,8 @@
     def arrive(b):
         settle(tap_like[b], tap_rs.at[b])
         core_copy(b).start()
-        if b == 0:
-            settle(ser_like, ser_rs.at[0])
+        for s in carried[b]:
+            settle(ser_like[s], ser_rs.at[s])
         core_copy(b).wait_recv()
 
     sign = (1 - 2 * g).astype(f32)
@@ -275,7 +275,7 @@
             def body(k, carry):
                 got = []
                 for p in range(n):
-                    value = ser[p, s, part] * tap[p, k, part]
+                    value = ser[s, p, part] * tap[p, k, part]
                     got.append((value * sign if p % 2 else value, None))
                 out = butterfly(got)
                 for u in range(half):
@@ -307,26 +307,27 @@
         one, two = tap[p, early[0]], tap[p, early[1]]
         new = []
         for s in range(mine):
-            a, b = ser[p, s] * one, ser[p, s] * two
+            a, b = ser[s, p] * one, ser[s, p] * two
             new.append(total[s] + (a * a + b * b))
         return tuple(new)
 
     for b in batches:
         arrive(b)
         front(0, b)
-        z_start(0, b)
-        if max(early) < places[b] + cores * sizes[b] and max(early) >= places[b]:
+        if b == len(sizes) - 1:
             total = lax.fori_loop(0, n, energy, tuple(jnp.zeros((sub_rows, LANES), f32) for _ in range(mine)))
             for s in range(mine):
                 en_out[s : s + 1] = jnp.sum(total[s], axis=0, keepdims=True)
             for dh in range(1, half):
                 en_copy(dh).start()
+        z_start(0, b)
     for s in range(1, mine):
         for b in batches:
             front(s, b)
             z_start(s, b)
 
-    settle(ser_like, ser_ss.at[0])
+    for s in range(mine):
+        settle(ser_like[s], ser_ss.at[s])
     for b in batches:
         settle(tap_like[b], tap_ss.at[b])
         core_copy(b).wait_send()
@@ -380,30 +381,38 @@
 
         lax.fori_loop(places[b] // 2, (places[b] + cores * sizes[b]) // 2, body, 0)
 
-    def combine(s, variance):
+    def measure(s, variance):
         def body(i, total):
+            at = pl.ds(pl.multiple_of(i * CHUNK, CHUNK), CHUNK)
+            powers = []
+            for k in range(tapers):
+                re, im = spec[0, k, at], spec[1, k, at]
+                powers.append(re * re + im * im)
+                power[s, k, at] = powers[k]
+            new = refine(0.5 * (powers[early[0]] + powers[early[1]]), powers, keep, variance)
+            est[s, at] = new
+            return total + new * weigh[at]
+
+        return lax.fori_loop(0, tall // CHUNK, body, jnp.zeros((CHUNK, LANES), f32))
+
+    def combine(s):
+        def body(i, carry):
             at = pl.ds(pl.multiple_of(i * CHUNK, CHUNK), CHUNK)
             re = [spec[0, k, at] for k in range(tapers)]
             im = [spec[1, k, at] for k in range(tapers)]
             sums = [None] * terms
-            powers = []
             pair = 0
             for j in range(tapers):
                 for k in range(j, tapers):
-                    both = re[j] * re[k] + im[j] * im[k]
-                    if j == k:
-                        powers.append(both)
-                        power[s, k, at] = both
+                    both = power[s, k, at] if j == k else re[j] * re[k] + im[j] * im[k]
                     for t in range(terms):
                         sums[t] = add(sums[t], pairs[t, pair] * both)
                     pair += 1
             for t in range(terms):
                 qi[s, t, at] = sums[t]
-            new = refine(0.5 * (powers[early[0]] + powers[early[1]]), powers, keep, variance)
-            est[s, at] = new
-            return total + new * weigh[at]
-
-        return lax.fori_loop(0, tall // CHUNK, body, jnp.zeros((CHUNK, LANES), f32))
+            return carry
+
+        lax.fori_loop(0, tall // CHUNK, body, 0)
 
     def sweep(s, variance):
         def body(i, total):
@@ -438,12 +447,13 @@
     def spec_copy(s):
         return remote(spec_out.at[s], spec_ref.at[g * mine + s], so_ss.at[0], so_rs.at[0], partner)
 
-    def outputs_qi(s, which):
-        for t in which:
+    def outputs_qi(s):
+        for t in range(terms):
             own, sent = assemble(qi.at[s, t])
-            qi_ref[g * mine + s, t] = own
             qi_out[s, t] = sent
             qi_copy(s, t).start()
+            qi_own[s, t] = own
+            pltpu.make_async_copy(qi_own.at[s, t], qi_ref.at[g * mine + s, t], own_sem.at[0]).start()
 
     totals = []
     for s in range(mine):
@@ -452,19 +462,22 @@
             transform(s, b)
         if s == 0:
             variance0 = first_variance()
-        totals.append(combine(s, variance0[s]))
-        if s < mine - 1:
-            outputs_qi(s, range(terms))
+        totals.append(measure(s, variance0[s]))
+        if s == mine - 1:
+            share(0, totals)
+        combine(s)
+        outputs_qi(s)
     for it in range(1, ITERS):
-        share(it - 1, totals)
-        outputs_qi(mine - 1, range(terms * (it - 1) // (ITERS - 1), terms * it // (ITERS - 1)))
+        if it > 1:
+            share(it - 1, totals)
         variance = collect(it - 1)
         totals = [sweep(s, variance[s]) for s in range(mine)]
     for s in range(mine):
         own, sent = assemble(est.at[s])
-        spec_ref[g * mine + s] = own
         spec_out[s] = sent
         spec_copy(s).start()
+        spec_own[s] = own
+        pltpu.make_async_copy(spec_own.at[s], spec_ref.at[g * mine + s], own_sem.at[1]).start()
 
     for s in range(mine):
         for b in batches:
@@ -474,13 +487,26 @@
     for s in range(mine):
         settle(qi_out.at[s], qo_rs.at[s])
         settle(qi_out.at[s], qo_ss.at[s])
+    settle(qi_own, own_sem.at[0])
+    settle(spec_own, own_sem.at[1])
     settle(spec_out, so_rs.at[0])
     settle(spec_out, so_ss.at[0])
 
 
-def hand_kernel(spec_ref, qi_ref, spec_out, qi_out):
-    spec_out[...] = spec_ref[...]
-    qi_out[...] = qi_ref[...]
+def hand_kernel(spec_ref, qi_ref, spec_out, qi_out, spec_held, qi_held, in_sem, out_sem):
+    sets = ((spec_ref, spec_held, spec_out), (qi_ref, qi_held, qi_out))
+    moves = []
+    for i, (src, held, dst) in enumerate(sets):
+        for s in range(src.shape[0]):
+            enter = pltpu.make_async_copy(src.at[s], held.at[s], in_sem.at[i, s])
+            leave = pltpu.make_async_copy(held.at[s], dst.at[s], out_sem.at[i, s])
+            enter.start()
+            moves.append((enter, leave))
+    for enter, leave in moves:
+        enter.wait()
+        leave.start()
+    for _, leave in moves:
+        leave.wait()
 
 
 def local(cores, series, tapers, concentration, qi_weights):
@@ -495,7 +521,6 @@
     sizes = (1,) * (taper_count // cores)
     f32 = jnp.float32
     bf16 = jnp.bfloat16
-    vmem = pl.BlockSpec(memory_space=pltpu.VMEM)
     smem = pl.BlockSpec(memory_space=pltpu.SMEM)
     hbm = pl.BlockSpec(memory_space=pltpu.HBM)
     dma = pltpu.SemaphoreType.DMA
@@ -507,14 +532,14 @@
         functools.partial(fused_kernel, n, cores, sizes),
         out_shape=shapes,
         in_specs=[hbm, hbm, smem, smem],
-        out_specs=(vmem, vmem),
+        out_specs=(hbm, hbm),
         scratch_shapes=[
             pltpu.VMEM(series.shape, f32),
             pltpu.VMEM(tapers.shape, f32),
             pltpu.VMEM((2, 8 * rows, LANES), f32),
             pltpu.VMEM((count, half, sub_rows, LANES), f32),
             pltpu.VMEM((taper_count, half, sub_rows, LANES), f32),
-            pltpu.VMEM((n, mine, sub_rows, LANES), f32),
+            pltpu.VMEM((mine, n, sub_rows, LANES), f32),
             pltpu.VMEM((n, taper_count, sub_rows, LANES), f32),
             pltpu.VMEM((half, mine, taper_count, 2, sub_rows, LANES), f32),
             pltpu.VMEM((mine, taper_count, 2, half, sub_rows, LANES), f32),
@@ -532,9 +557,11 @@
             pltpu.VMEM((mine, terms, tall, LANES), f32),
             pltpu.VMEM((mine, LANES, rows), f32),
             pltpu.VMEM((mine, terms, LANES, rows), f32),
+            pltpu.VMEM((mine, LANES, rows), f32),
+            pltpu.VMEM((mine, terms, LANES, rows), f32),
             pltpu.SMEM((terms, taper_count * (taper_count + 1) // 2), f32),
             pltpu.VMEM((2, rows, LANES), f32),
-            dma((1,)), dma((1,)),
+            dma((mine,)), dma((mine,)),
             dma((len(sizes),)), dma((len(sizes),)),
             dma((len(sizes),)), dma((len(sizes),)),
             dma((1,)), dma((1,)),
@@ -542,12 +569,16 @@
             dma((ITERS - 1,)), dma((ITERS - 1,)),
             dma((mine,)), dma((mine,)),
             dma((1,)), dma((1,)),
-            dma((2,)),
+            dma((2,)), dma((2,)),
         ],
         compiler_params=pltpu.CompilerParams(collective_id=0, has_side_effects=True),
     )(series, tapers, concentration, qi_weights.transpose(1, 0, 2))
     spectrum, qi_terms = pl.pallas_call(
-        hand_kernel, out_shape=shapes, in_specs=[vmem, vmem], out_specs=(vmem, vmem)
+        hand_kernel,
+        out_shape=shapes,
+        in_specs=[hbm, hbm],
+        out_specs=(hbm, hbm),
+        scratch_shapes=[pltpu.VMEM(shape.shape, f32) for shape in shapes] + [dma((2, count)), dma((2, count))],
     )(*outs)
     return (
         spectrum.reshape(count, 1, local_len),

time: 86.3 us -> 82.3 us (0.954)
  Pallas kernels: 85.4 us -> 80.6 us
    pallas_call x1, Pallas kernels: 83 us -> 78.4 us  [local(): pl.pallas_call(functools.partial(fused_kernel, n, cores, sizes), out_shap...]
where the time goes in v4:
time: 82.3 us; the launch traced here: 81.3 us
  Pallas kernels  80.6 us (98%)
    pallas_call x1, Pallas kernels, local(): pl.pallas_call(functools.partial(fused_kernel, n, cores, sizes), out_shap...  78.4 us
    pallas_call x1, Pallas kernels, local(): pl.pallas_call(hand_kernel, out_shape=shapes, in_specs=[hbm, hbm], out_sp...  2.19 us

profile of v4, /device:TPU:0, one launch (start us, length us, event | category | flops | bytes accessed | tf_op | source)
XLA Modules:
  0.0 81.3 jit_solution(3989478839679290946)
XLA Ops:
  0.6 78.4 %shard_map.59 = (f32[4,128,128]{2,1,0:T(8,128)}, f32[4,4,128,128]{3,2,1,0:T(8,128)}) custom-call(f32[4,16384]{1,0:T(4,128)} %series_hbm.1, f32[10,16384]{1,0:T(8,128)} %tapers_hbm.1, f32[10]{0:T(128)} %keep_ref.1, f32[10,4,10]{2,1,0:T(4,128)} %bitcast.3), custom_call_target="tpu_custom_call" | custom-call | tf_op jit(solution)/shard_map/pallas_call | solution.py:531
  79.1 2.2 %shard_map.60 = (f32[4,128,128]{2,1,0:T(8,128)}, f32[4,4,128,128]{3,2,1,0:T(8,128)}) custom-call(f32[4,128,128]{2,1,0:T(8,128)} %get-tuple-element.6.spec_ref, f32[4,4,128,128]{3,2,1,0:T(8,128)} %get-tuple-element.7.qi_ref), custom_call_target="tpu_custom_call" | custom-call | tf_op jit(solution)/shard_map/pallas_call | solution.py:576

commit v5 on v4

--- a/solution.py
+++ b/solution.py
@@ -447,8 +447,8 @@
     def spec_copy(s):
         return remote(spec_out.at[s], spec_ref.at[g * mine + s], so_ss.at[0], so_rs.at[0], partner)
 
-    def outputs_qi(s):
-        for t in range(terms):
+    def outputs_qi(s, which):
+        for t in which:
             own, sent = assemble(qi.at[s, t])
             qi_out[s, t] = sent
             qi_copy(s, t).start()
@@ -460,13 +460,15 @@
         for b in batches:
             settle(z_like[s][b], z_rs.at[s, b])
             transform(s, b)
+            if s:
+                outputs_qi(s - 1, [t for t in range(1, terms) if min(t, len(sizes) - 1) == b])
         if s == 0:
             variance0 = first_variance()
         totals.append(measure(s, variance0[s]))
         if s == mine - 1:
             share(0, totals)
         combine(s)
-        outputs_qi(s)
+        outputs_qi(s, range(terms) if s == mine - 1 else [0])
     for it in range(1, ITERS):
         if it > 1:
             share(it - 1, totals)

time: 82.3 us -> 80.9 us (0.983)
  no operation moved by 1% of the time
where the time goes in v5:
time: 80.9 us; the launch traced here: 80.7 us
  Pallas kernels  80.1 us (99%)
    pallas_call x1, Pallas kernels, local(): pl.pallas_call(functools.partial(fused_kernel, n, cores, sizes), out_shap...  77.9 us
    pallas_call x1, Pallas kernels, local(): pl.pallas_call(hand_kernel, out_shape=shapes, in_specs=[hbm, hbm], out_sp...  2.19 us

profile of v5, /device:TPU:0, one launch (start us, length us, event | category | flops | bytes accessed | tf_op | source)
XLA Modules:
  0.0 80.7 jit_solution(17346230695403701714)
XLA Ops:
  0.6 77.9 %shard_map.59 = (f32[4,128,128]{2,1,0:T(8,128)}, f32[4,4,128,128]{3,2,1,0:T(8,128)}) custom-call(f32[4,16384]{1,0:T(4,128)} %series_hbm.1, f32[10,16384]{1,0:T(8,128)} %tapers_hbm.1, f32[10]{0:T(128)} %keep_ref.1, f32[10,4,10]{2,1,0:T(4,128)} %bitcast.3), custom_call_target="tpu_custom_call" | custom-call | tf_op jit(solution)/shard_map/pallas_call | solution.py:533
  78.5 2.2 %shard_map.60 = (f32[4,128,128]{2,1,0:T(8,128)}, f32[4,4,128,128]{3,2,1,0:T(8,128)}) custom-call(f32[4,128,128]{2,1,0:T(8,128)} %get-tuple-element.6.spec_ref, f32[4,4,128,128]{3,2,1,0:T(8,128)} %get-tuple-element.7.qi_ref), custom_call_target="tpu_custom_call" | custom-call | tf_op jit(solution)/shard_map/pallas_call | solution.py:578
